TPU v7x, 32 devices: a whole 2x2x4 slice. The times are simulated.
32 devices in a mesh: dp: 2 (over x), vocab: 16 (over z, y, core).
Axes of the slice: x: 2, y: 2, z: 4, core: 2. Of those that a mesh axis runs over, the one named last changes fastest.
Arguments:
- hidden: bfloat16 [160, 4608], P('dp'), may hold values from -30 to 30
- head_weight: bfloat16 [4608, 16384], P(None, ('dp', 'vocab')), may hold values from -0.09375 to 0.09375
- drafts: int32 [32, 4], replicated, may hold values from 0 to 16383
- cutoffs: int32 [32, 4], P('dp'), may hold values from -30720 to -18433
Outputs:
- log_norm: float32 [32, 5], P('dp')
- draft_logprob: float32 [32, 4], P('dp')
- expected_accept: float32 [32], P('dp')
- z_loss: float32 [], replicated
All inputs are finite; a program needn't handle non-finite values.
Results may differ from a plain program's by a relative error of at most 0.0003.
Values may be sent and summed in bfloat16 or wider, within the bound.
No kernel may reach another device: no remote copies, remote signals or barrier semaphores. Data moves between devices by JAX's collectives and lax.ppermute only.
A program may use at most 64 MiB of HBM per device.

v0:
```python
import jax
import jax.numpy as jnp
from jax import lax
from jax.sharding import PartitionSpec as P

DRAFTS = 4
POSITIONS = 5


SOFT_CAP = 30.0
Z_WEIGHT = 0.001


def local(hidden, head_weight, drafts, cutoffs):
    vocab_devices = lax.axis_size("vocab")
    shard_index = lax.axis_index("dp") * vocab_devices + lax.axis_index("vocab")
    shard_width = head_weight.shape[1]
    offset = shard_index * shard_width
    sentinel = jnp.full((drafts.shape[0], 1), -1, jnp.int32)
    draft_rows = jnp.concatenate([drafts, sentinel], axis=1).reshape(-1)
    local_ids = jnp.where(draft_rows >= 0, draft_rows - offset, -1)
    columns = lax.broadcasted_iota(jnp.int32, (1, shard_width), 1)
    logits = jnp.dot(
        lax.all_gather(hidden, "dp", axis=0, tiled=True),
        head_weight,
        preferred_element_type=jnp.float32,
    )
    capped = SOFT_CAP * jnp.tanh(logits / SOFT_CAP)
    exp_total = jnp.sum(jnp.exp(capped), axis=1)
    picked = jnp.sum(jnp.where(columns == local_ids[:, None], capped, 0.0), axis=1)
    partial_value = jnp.stack([exp_total, picked], 0)
    exp_total = partial_value[0]
    picked = partial_value[1]
    own_rows = hidden.shape[0]
    exp_total, picked = lax.psum((exp_total, picked), ("dp", "vocab"))
    log_total = jnp.log(exp_total)
    z_loss = Z_WEIGHT * jnp.mean(log_total * log_total)
    first_own = lax.axis_index("dp") * own_rows
    log_total = lax.dynamic_slice_in_dim(log_total, first_own, own_rows, 0)
    picked = lax.dynamic_slice_in_dim(picked, first_own, own_rows, 0)
    log_norm = log_total.reshape(-1, POSITIONS)
    picks = picked.reshape(-1, POSITIONS)
    draft_logprob = picks[:, :DRAFTS] - log_norm[:, :DRAFTS]
    accept = jax.nn.sigmoid(draft_logprob - cutoffs.astype(jnp.float32) / 1024.0)
    expected_accept = jnp.sum(jnp.cumprod(accept, axis=1), axis=1)
    return (log_norm, draft_logprob, expected_accept, z_loss)


def solution(mesh):
    in_specs = (P("dp", None), P(None, ("dp", "vocab")), P(), P("dp", None))
    out_specs = (P("dp", None), P("dp", None), P("dp"), P())
    return jax.shard_map(local, mesh=mesh, in_specs=in_specs, out_specs=out_specs, check_vma=False)
```

profile of v0, /device:TPU:0, one launch (start us, length us, event | category | flops | bytes accessed | tf_op | source)
XLA Modules:
  0.0 93.3 jit_solution(8154429625107893591)
XLA Ops:
  7.2 0.0 all-gather.2.cloned.1.call-start
  7.2 0.7 all-gather.2.cloned.1.call-update
  7.9 0.7 fusion.2
  8.6 0.1 copy.11
  8.7 0.1 select_n.21
  8.8 0.8 copy.12
  9.6 28.8 %all-gather.2.cloned.1.call-done = bf16[160,4608]{1,0:T(8,128)(2,1)} async-done(((bf16[80,4608]{1,0:T(8,128)(2,1)}), bf16[160,4608]{1,0:T(8,128)(2,1)}) %all-gather.2.cloned.1.call-update) | async-done | bytes 1474576 | tf_op jit(solution)/shard_map/all_gather | solution.py:24
  38.3 3.9 %select_reduce_fusion = (f32[160]{0:T(256)S(1)}, f32[160]{0:T(256)S(1)}) fusion(s32[160]{0:T(256)S(1)} %select_n.21, bf16[160,4608]{1,0:T(8,128)(2,1)} %all-gather.2.cloned.1.call-done, bf16[4608,512]{1,0:T(8,128)(2,1)} %param.5), kind=kOutput, calls=%fused_computation.3 | convolution fusion | flops 755465984 | bytes 6195072 | tf_op jit(solution)/shard_map/dot_general | solution.py:23
  42.3 39.3 %all-reduce.1 = (f32[160]{0:T(256)S(1)}, f32[160]{0:T(256)S(1)}) all-reduce(f32[160]{0:T(256)S(1)} %get-tuple-element.13, f32[160]{0:T(256)S(1)} %get-tuple-element.12), channel_id=1, replica_groups=mesh['dp'=2,'vocab'=16] {'dp','vocab'}, use_global_device_ids=true, to_apply=%region_1.2 | all-reduce | flops 320 | bytes 2560 | tf_op jit(solution)/shard_map/psum | solution.py:35
  81.6 0.6 multiply_reduce_fusion
  82.2 0.1 dynamic_slice.6
  82.3 0.1 reshape.31
  82.4 0.1 dynamic_slice.7
  82.4 0.1 reshape.32
  82.5 0.7 copy.13
  83.2 0.7 copy.14
  83.9 0.2 reduce_window.9
  84.0 0.6 reduce_sum.38
  (1 shorter events, 0.0 us)
Async XLA Ops:
  7.2 31.2 %all-gather.2.cloned.1.call-start = ((), (), s32[]{:S(2)}) async-start(), calls=%async_computation | async-start | bytes 2211840 | tf_op jit(solution)/shard_map/all_gather | solution.py:24
Sparse Core Ops, SparseCore 0:
  9.5 28.7 all-gather.1
where the time goes:
time: 93.7 us; the launch traced here: 93.3 us
  blocking collectives  39.3 us (42%)
  waiting for transfers between devices  29.5 us (31%)
  between operations  15.8 us (17%)
  matrix products  3.92 us (4%)
  local copies, waits for them, and re-layouts  2.61 us (3%)
  other arithmetic  2.09 us (2%)
    psum x1, blocking collectives, local(): exp_total, picked = lax.psum((exp_total, picked), ('dp', 'vocab'))  39.3 us
    all_gather x1, waiting for transfers between devices, local(): lax.all_gather(hidden, 'dp', axis=0, tiled=True)  28.8 us
    dot_general x1, matrix products, local(): jnp.dot(lax.all_gather(hidden, 'dp', axis=0, tiled=True), head_weight, pr...  3.92 us
    unnamed x3, local copies, waits for them, and re-layouts  2.11 us
  transfers between devices with their start and end apart: 1, of which 1 were waited for; matrix products, arithmetic and copies ran while one was open for 2% of the time, Pallas kernels for 0%

commit v1 on v0

v1 whole, which is shorter than its diff:
```python
import functools

import jax
import jax.numpy as jnp
from jax import lax
from jax.experimental import pallas as pl
from jax.experimental.pallas import tpu as pltpu
from jax.sharding import PartitionSpec as P

DRAFTS = 4
POSITIONS = 5
SOFT_CAP = 30.0
Z_WEIGHT = 0.001
LANES = 128
GRANT = 16 * 2**20
VMEM = pl.BlockSpec(memory_space=pltpu.VMEM)


def tile_width(seqs):
    return -(-2 * seqs // LANES) * LANES


def row_ids(drafts, rows, first_seq):
    shape = (rows, drafts.shape[1])
    seq = lax.broadcasted_iota(jnp.int32, shape, 1) - first_seq
    target = lax.broadcasted_iota(jnp.int32, shape, 0) - seq * POSITIONS
    shifted = (drafts + 1).astype(jnp.float32)
    picked = jnp.zeros(shape, jnp.float32)
    for p in range(DRAFTS):
        picked = jnp.where(target == p, shifted[p : p + 1], picked)
    return jnp.sum(picked, axis=1, keepdims=True).astype(jnp.int32) - 1


def contribution(logits, drafts, first_seq):
    rows, width = logits.shape
    seqs = drafts.shape[1]
    shard = lax.axis_index("dp") * lax.axis_size("vocab") + lax.axis_index("vocab")
    ids = row_ids(drafts, rows, first_seq) - shard * width
    capped = SOFT_CAP * jnp.tanh(logits * (1.0 / SOFT_CAP))
    totals = jnp.sum(jnp.exp(capped), axis=1, keepdims=True)
    columns = lax.broadcasted_iota(jnp.int32, (rows, width), 1)
    picks = jnp.sum(jnp.where(columns == ids, capped, 0.0), axis=1, keepdims=True)
    shape = (rows, tile_width(seqs))
    lane = lax.broadcasted_iota(jnp.int32, shape, 1)
    row = lax.broadcasted_iota(jnp.int32, shape, 0)
    values = jnp.where(lane < seqs, totals, picks)
    seq = jnp.where(lane < seqs, lane, lane - seqs) - first_seq
    target = row - seq * POSITIONS
    position = lax.broadcasted_iota(jnp.int32, (8, shape[1]), 0)
    tile = jnp.zeros((8, shape[1]), jnp.float32)
    for p in range(POSITIONS):
        line = jnp.sum(jnp.where(target == p, values, 0.0), axis=0, keepdims=True)
        tile = jnp.where(position == p, line, tile)
    return tile


def own_kernel(hidden_ref, weight_ref, drafts_ref, tile_ref):
    own_seqs = hidden_ref.shape[0] // POSITIONS
    first_seq = lax.axis_index("dp") * own_seqs
    logits = jnp.dot(hidden_ref[...], weight_ref[...], preferred_element_type=jnp.float32)
    tile_ref[...] = contribution(logits, drafts_ref[...], first_seq)


def other_kernel(shift, copies, near_ref, far_ref, weight_ref, drafts_ref, before_ref, out_ref):
    own_seqs = near_ref.shape[0] // POSITIONS
    dp = lax.axis_size("dp")
    source = lax.rem(lax.axis_index("dp") + dp - shift, dp)
    depth = near_ref.shape[1]
    core = lax.rem(lax.axis_index("vocab"), 2)
    near = pl.ds(pl.multiple_of(core * depth, depth), depth)
    far = pl.ds(pl.multiple_of((1 - core) * depth, depth), depth)
    logits = jnp.dot(near_ref[...], weight_ref[near, :], preferred_element_type=jnp.float32)
    logits += jnp.dot(far_ref[...], weight_ref[far, :], preferred_element_type=jnp.float32)
    tile = contribution(logits, drafts_ref[...], source * own_seqs) + before_ref[...]
    out_ref[...] = jnp.broadcast_to(tile[None], (copies,) + tile.shape)


def tail_kernel(seqs, parts_ref, cutoffs_ref, norm_ref, logprob_ref, expected_ref, loss_ref):
    own_seqs = cutoffs_ref.shape[1]
    width = parts_ref.shape[2]
    tile = jnp.sum(parts_ref[...], axis=0)
    position = lax.broadcasted_iota(jnp.int32, tile.shape, 0)
    lane = lax.broadcasted_iota(jnp.int32, tile.shape, 1)
    log_total = jnp.log(jnp.where((position < POSITIONS) & (lane < seqs), tile, 1.0))
    squares = jnp.sum(jnp.sum(log_total * log_total, axis=1, keepdims=True), axis=0, keepdims=True)
    loss_ref[...] = squares * (Z_WEIGHT / (seqs * POSITIONS))
    first = lax.axis_index("dp") * own_seqs
    log_norm = pltpu.roll(log_total, lax.rem(width - first, width), 1)
    picks = pltpu.roll(tile, lax.rem(2 * width - seqs - first, width), 1)
    norm_ref[...] = log_norm[:POSITIONS, :own_seqs]
    logprob = picks[:DRAFTS, :own_seqs] - log_norm[:DRAFTS, :own_seqs]
    logprob_ref[...] = logprob
    accept = jax.nn.sigmoid(logprob - cutoffs_ref[...].astype(jnp.float32) / 1024.0)
    product = accept[0:1]
    expected = product
    for p in range(1, DRAFTS):
        product = product * accept[p : p + 1]
        expected = expected + product
    expected_ref[...] = expected


def local(hidden, head_weight, drafts, cutoffs):
    dp, vocab = lax.axis_size("dp"), lax.axis_size("vocab")
    rows, depth = hidden.shape
    width = head_weight.shape[1]
    seqs = drafts.shape[0]
    own_seqs = rows // POSITIONS
    tile = jax.ShapeDtypeStruct((8, tile_width(seqs)), jnp.float32)
    half = depth // 2
    core = lax.rem(lax.axis_index("vocab"), 2)
    mine = lax.dynamic_slice_in_dim(hidden, core * half, half, 1)
    swap = [(i, i ^ 1) for i in range(vocab)]
    near = [lax.ppermute(mine, "dp", [(i, (i + k) % dp) for i in range(dp)]) for k in range(1, dp)]
    cost = pl.CostEstimate(
        flops=2 * rows * depth * width,
        bytes_accessed=2 * depth * (rows + width),
        transcendentals=2 * rows * width,
    )
    tokens = drafts.T
    parts = pl.pallas_call(
        own_kernel,
        out_shape=tile,
        in_specs=[VMEM] * 3,
        out_specs=VMEM,
        cost_estimate=cost,
        compiler_params=pltpu.CompilerParams(vmem_limit_bytes=GRANT),
        name="own_rows",
    )(hidden, head_weight, tokens)
    near, parts = lax.optimization_barrier((near, parts))
    far = [lax.ppermute(block, "vocab", swap) for block in near]
    for k in range(1, dp):
        copies = dp * vocab if k == dp - 1 else 1
        parts = pl.pallas_call(
            functools.partial(other_kernel, k, copies),
            out_shape=jax.ShapeDtypeStruct((copies,) + tile.shape, jnp.float32),
            in_specs=[VMEM] * 5,
            out_specs=VMEM,
            cost_estimate=cost,
            compiler_params=pltpu.CompilerParams(vmem_limit_bytes=GRANT),
            name="other_rows",
        )(near[k - 1], far[k - 1], head_weight, tokens, parts)
        if copies == 1:
            parts = parts[0]
    parts = lax.all_to_all(parts, ("dp", "vocab"), 0, 0)
    log_norm, logprob, expected, loss = pl.pallas_call(
        functools.partial(tail_kernel, seqs),
        out_shape=(
            jax.ShapeDtypeStruct((POSITIONS, own_seqs), jnp.float32),
            jax.ShapeDtypeStruct((DRAFTS, own_seqs), jnp.float32),
            jax.ShapeDtypeStruct((1, own_seqs), jnp.float32),
            jax.ShapeDtypeStruct((1, 1), jnp.float32),
        ),
        in_specs=[VMEM] * 2,
        out_specs=(VMEM,) * 4,
        compiler_params=pltpu.CompilerParams(vmem_limit_bytes=GRANT),
        name="tail",
    )(parts, cutoffs.T)
    return log_norm.T, logprob.T, expected.reshape(own_seqs), loss.reshape(())


def solution(mesh):
    in_specs = (P("dp", None), P(None, ("dp", "vocab")), P(), P("dp", None))
    out_specs = (P("dp", None), P("dp", None), P("dp"), P())
    return jax.shard_map(local, mesh=mesh, in_specs=in_specs, out_specs=out_specs, check_vma=False)
```

time: 93.7 us -> 31.1 us (0.33)
  blocking collectives: 39.3 us -> 14.1 us
  waiting for transfers between devices: 29.5 us -> 5.07 us
  between operations: 15.8 us -> 0.67 us
  matrix products: 3.92 us -> 0 us
  starting transfers between devices: 0.04 us -> 3.03 us
  Pallas kernels: 0 us -> 2.82 us
  local copies, waits for them, and re-layouts: 2.61 us -> 5.16 us
  other arithmetic: 2.09 us -> 0 us
    psum x1 -> x0, blocking collectives: 39.3 us -> none  [local(): exp_total, picked = lax.psum((exp_total, picked), ('dp', 'vocab'))]
    all_gather x1 -> x0, waiting for transfers between devices: 28.8 us -> none  [local(): lax.all_gather(hidden, 'dp', axis=0, tiled=True)]
    all_to_all x0 -> x1, blocking collectives: none -> 14.1 us  [local(): parts = lax.all_to_all(parts, ('dp', 'vocab'), 0, 0)]
    ppermute x0 -> x2, waiting for transfers between devices: none -> 5.07 us  [the longest x1 3.39 us: local(): lax.ppermute(mine, 'dp', [(i, (i + k) % dp) for i in range(dp)])]
    dot_general x1 -> x0, matrix products: 3.92 us -> none  [local(): jnp.dot(lax.all_gather(hidden, 'dp', axis=0, tiled=True), head_weight, pr...]
    ppermute x0 -> x2, starting transfers between devices: none -> 3.03 us  [the longest x1 3.03 us: local(): lax.ppermute(mine, 'dp', [(i, (i + k) % dp) for i in range(dp)])]
    pallas_call x0 -> x3, Pallas kernels: none -> 2.82 us  [the longest x1 1.06 us: local(): pl.pallas_call(functools.partial(other_kernel, k, copies), out_shape=jax....]
    unnamed x3 -> x10, local copies, waits for them, and re-layouts: 2.11 us -> 4.14 us
  transfers between devices with their start and end apart: 1 -> 2, of which waited for: 1 -> 2; matrix products, arithmetic and copies ran while one was open for 2% -> 0% of each run, Pallas kernels for 0% -> 3%
where the time goes in v1:
time: 31.1 us; the launch traced here: 30.9 us
  blocking collectives  14.1 us (45%)
  local copies, waits for them, and re-layouts  5.16 us (17%)
  waiting for transfers between devices  5.07 us (16%)
  starting transfers between devices  3.03 us (10%)
  Pallas kernels  2.82 us (9%)
  between operations  0.67 us (2%)
    all_to_all x1, blocking collectives, local(): parts = lax.all_to_all(parts, ('dp', 'vocab'), 0, 0)  14.1 us
    unnamed x10, local copies, waits for them, and re-layouts  4.14 us
    ppermute x1, waiting for transfers between devices, local(): lax.ppermute(mine, 'dp', [(i, (i + k) % dp) for i in range(dp)])  3.39 us
    ppermute x1, starting transfers between devices, local(): lax.ppermute(mine, 'dp', [(i, (i + k) % dp) for i in range(dp)])  3.03 us
    ppermute x1, waiting for transfers between devices, local(): far = [lax.ppermute(block, 'vocab', swap) for block in near]  1.68 us
    pallas_call x1, Pallas kernels, local(): pl.pallas_call(functools.partial(other_kernel, k, copies), out_shape=jax....  1.06 us
    pallas_call x1, Pallas kernels, local(): pl.pallas_call(own_kernel, out_shape=tile, in_specs=[VMEM] * 3, out_specs...  1.05 us
    dynamic_slice x1, local copies, waits for them, and re-layouts, local(): mine = lax.dynamic_slice_in_dim(hidden, core * half, half, 1)  1.02 us
  transfers between devices with their start and end apart: 2, of which 2 were waited for; matrix products, arithmetic and copies ran while one was open for 0% of the time, Pallas kernels for 3%

profile of v1, /device:TPU:0, one launch (start us, length us, event | category | flops | bytes accessed | tf_op | source)
XLA Modules:
  0.0 30.9 jit_solution(11312950460014169314)
XLA Ops:
  0.6 1.0 %constant_dynamic-slice_fusion = bf16[80,2304]{1,0:T(8,128)(2,1)S(1)} fusion(bf16[80,4608]{1,0:T(8,128)(2,1)} %hidden_ref.1, s32[]{:T(128)S(6)} %select_n.3), kind=kLoop, calls=%fused_computation | loop fusion | bytes 737284 | tf_op jit(solution)/shard_map/dynamic_slice | solution.py:111
  1.7 3.0 %collective-permute-start = (bf16[80,2304]{1,0:T(8,128)(2,1)S(1)}, bf16[80,2304]{1,0:T(8,128)(2,1)S(1)}, u32[]{:S(2)}, u32[]{:S(2)}) collective-permute-start(bf16[80,2304]{1,0:T(8,128)(2,1)S(1)} %constant_dynamic-slice_fusion), channel_id=1, source_target_pairs={{0,16},{16,0},{1,17},{17,1},{2,18},{18,2},{3,19},{19,3},{4,20},{20... | collective-permute-start | bytes 1105928 | tf_op jit(solution)/shard_map/ppermute | solution.py:113
  4.7 0.0 copy-start
  4.7 2.3 %copy-done = bf16[4608,512]{1,0:T(8,128)(2,1)S(1)} copy-done((bf16[4608,512]{1,0:T(8,128)(2,1)S(1)}, bf16[4608,512]{1,0:T(8,128)(2,1)}, u32[]{:S(2)}) %copy-start) | copy-done | bytes 4718616
  7.0 0.0 copy-start.2
  7.0 1.1 %copy-done.2 = bf16[80,4608]{1,0:T(8,128)(2,1)S(1)} copy-done((bf16[80,4608]{1,0:T(8,128)(2,1)S(1)}, bf16[80,4608]{1,0:T(8,128)(2,1)}, u32[]{:S(2)}) %copy-start.2) | copy-done | bytes 737304
  8.1 0.0 copy-start.3
  8.1 0.7 %copy-done.3 = s32[32,4]{0,1:T(4,128)S(1)} copy-done((s32[32,4]{0,1:T(4,128)S(1)}, s32[32,4]{0,1:T(4,128)}, u32[]{:S(2)}) %copy-start.3) | copy-done | bytes 536
  8.8 0.0 copy-start.1
  8.8 0.0 copy-start.4
  8.8 1.1 %own_rows.1.before_ref = f32[8,128]{1,0:T(8,128)S(1)} custom-call(bf16[80,4608]{1,0:T(8,128)(2,1)S(1)} %copy-done.2, bf16[4608,512]{1,0:T(8,128)(2,1)S(1)} %copy-done, s32[4,32]{1,0:T(4,128)S(1)} %bitcast.6), custom_call_target="tpu_custom_call" | custom-call | flops 377487360 | bytes 5455872 | tf_op jit(solution)/shard_map/own_rows/pallas_call | solution.py:120
  9.9 3.4 %collective-permute-done.near_ref = bf16[80,2304]{1,0:T(8,128)(2,1)S(1)} collective-permute-done((bf16[80,2304]{1,0:T(8,128)(2,1)S(1)}, bf16[80,2304]{1,0:T(8,128)(2,1)S(1)}, u32[]{:S(2)}, u32[]{:S(2)}) %collective-permute-start) | collective-permute-done | bytes 368672 | tf_op jit(solution)/shard_map/ppermute | solution.py:113
  13.3 0.0 collective-permute-start.1
  13.3 1.7 %collective-permute-done.1.far_ref = bf16[80,2304]{1,0:T(8,128)(2,1)S(1)} collective-permute-done((bf16[80,2304]{1,0:T(8,128)(2,1)S(1)}, bf16[80,2304]{1,0:T(8,128)(2,1)S(1)}, u32[]{:S(2)}, u32[]{:S(2)}) %collective-permute-start.1) | collective-permute-done | bytes 368672 | tf_op jit(solution)/shard_map/ppermute | solution.py:130
  15.0 0.0 copy-done.1
  15.0 1.1 %other_rows.1 = f32[32,8,128]{2,1,0:T(8,128)S(1)} custom-call(bf16[80,2304]{1,0:T(8,128)(2,1)S(1)} %collective-permute-done.near_ref, bf16[80,2304]{1,0:T(8,128)(2,1)S(1)} %collective-permute-done.1.far_ref, bf16[4608,512]{1,0:T(8,128)(2,1)S(1)} %copy-done.1, s32[4,32]{1,0:T(4,128)S(1)} %bitcast.7, f32[8,128]{1,0:T(8,128)S(1)} %own_rows.1.before_ref), custom_call_target="tpu_custom_call" | custom-call | flops 377487360 | bytes 5455872 | tf_op jit(solution)/shard_map/other_rows/pallas_call | solution.py:133
  16.0 14.1 %all_to_all.5.parts_ref = f32[32,8,128]{2,1,0:T(8,128)S(1)} all-to-all(f32[32,8,128]{2,1,0:T(8,128)S(1)} %other_rows.1), channel_id=1, replica_groups=mesh['dp'=2,'vocab'=16] {'dp','vocab'}, dimensions={0} | all-to-all | bytes 262144 | tf_op jit(solution)/shard_map/all_to_all | solution.py:144
  30.2 0.0 copy-done.4
  30.2 0.7 %tail.1 = (f32[5,16]{1,0:T(8,128)}, f32[4,16]{1,0:T(4,128)}, f32[1,16]{1,0:T(1,128)}, f32[1,1]{1,0:T(1,128)}) custom-call(f32[32,8,128]{2,1,0:T(8,128)S(1)} %all_to_all.5.parts_ref, s32[4,16]{1,0:T(4,128)S(1)} %bitcast.8), custom_call_target="tpu_custom_call" | custom-call | tf_op jit(solution)/shard_map/tail/pallas_call | solution.py:145
Async XLA Ops:
  1.7 11.6 %collective-permute-start = (bf16[80,2304]{1,0:T(8,128)(2,1)S(1)}, bf16[80,2304]{1,0:T(8,128)(2,1)S(1)}, u32[]{:S(2)}, u32[]{:S(2)}) collective-permute-start(bf16[80,2304]{1,0:T(8,128)(2,1)S(1)} %constant_dynamic-slice_fusion), channel_id=1, source_target_pairs={{0,16},{16,0},{1,17},{17,1},{2,18},{18,2},{3,19},{19,3},{4,20},{20... | collective-permute-start | bytes 1105928 | tf_op jit(solution)/shard_map/ppermute | solution.py:113
  4.7 2.3 %copy-start = (bf16[4608,512]{1,0:T(8,128)(2,1)S(1)}, bf16[4608,512]{1,0:T(8,128)(2,1)}, u32[]{:S(2)}) copy-start(bf16[4608,512]{1,0:T(8,128)(2,1)} %weight_ref.3) | copy-start | bytes 14155780
  7.0 1.1 %copy-start.2 = (bf16[80,4608]{1,0:T(8,128)(2,1)S(1)}, bf16[80,4608]{1,0:T(8,128)(2,1)}, u32[]{:S(2)}) copy-start(bf16[80,4608]{1,0:T(8,128)(2,1)} %hidden_ref.1) | copy-start | bytes 2211844
  8.1 0.7 %copy-start.3 = (s32[32,4]{0,1:T(4,128)S(1)}, s32[32,4]{0,1:T(4,128)}, u32[]{:S(2)}) copy-start(s32[32,4]{0,1:T(4,128)} %param.6) | copy-start | bytes 1540
  8.8 6.1 %copy-start.1 = (bf16[4608,512]{1,0:T(8,128)(2,1)S(1)}, bf16[4608,512]{1,0:T(8,128)(2,1)}, u32[]{:S(2)}) copy-start(bf16[4608,512]{1,0:T(8,128)(2,1)} %weight_ref.3) | copy-start | bytes 14155780
  8.8 21.3 %copy-start.4 = (s32[16,4]{0,1:T(4,128)S(1)}, s32[16,4]{0,1:T(4,128)}, u32[]{:S(2)}) copy-start(s32[16,4]{0,1:T(4,128)} %param.7) | copy-start | bytes 772
  13.3 1.7 %collective-permute-start.1 = (bf16[80,2304]{1,0:T(8,128)(2,1)S(1)}, bf16[80,2304]{1,0:T(8,128)(2,1)S(1)}, u32[]{:S(2)}, u32[]{:S(2)}) collective-permute-start(bf16[80,2304]{1,0:T(8,128)(2,1)S(1)} %collective-permute-done.near_ref), channel_id=1, source_target_pairs={{0,1},{1,0},{2,3},{3,2},{4,5},{5,4},{6,7},{7,6},{8,9},{9,8},{10,11... | collective-permute-start | bytes 1105928 | tf_op jit(solution)/shard_map/ppermute | solution.py:130

commit v2 on v1

v2 whole, which is shorter than its diff:
```python
import functools

import jax
import jax.numpy as jnp
from jax import lax
from jax.experimental import pallas as pl
from jax.experimental.pallas import tpu as pltpu
from jax.sharding import PartitionSpec as P

DRAFTS = 4
POSITIONS = 5
SOFT_CAP = 30.0
Z_WEIGHT = 0.001
LANES = 128
GRANT = 16 * 2**20
VMEM = pl.BlockSpec(memory_space=pltpu.VMEM)


def row_ids(drafts, rows, first_seq):
    shape = (rows, drafts.shape[1])
    seq = lax.broadcasted_iota(jnp.int32, shape, 1) - first_seq
    target = lax.broadcasted_iota(jnp.int32, shape, 0) - seq * POSITIONS
    shifted = (drafts + 1).astype(jnp.float32)
    picked = jnp.zeros(shape, jnp.float32)
    for p in range(DRAFTS):
        picked = jnp.where(target == p, shifted[p : p + 1], picked)
    return jnp.sum(picked, axis=1, keepdims=True).astype(jnp.int32) - 1


def spread(column, starts, lines):
    shape = (column.shape[0], LANES)
    offset = lax.broadcasted_iota(jnp.int32, shape, 0) - POSITIONS * lax.broadcasted_iota(jnp.int32, shape, 1)
    out = []
    for line in range(lines):
        values = jnp.zeros(shape, jnp.float32)
        for p, start in enumerate(starts):
            values = jnp.where(offset == POSITIONS * (line * LANES - start) + p, column, values)
        out.append(jnp.sum(values, axis=0, keepdims=True))
    return jnp.concatenate(out, axis=0)


def payload_lines(seqs, own_seqs):
    return -(-(POSITIONS * seqs + DRAFTS * own_seqs) // LANES)


def contribution(logits, drafts, source):
    rows, width = logits.shape
    seqs, own_seqs = drafts.shape[1], rows // POSITIONS
    shard = lax.axis_index("dp") * lax.axis_size("vocab") + lax.axis_index("vocab")
    ids = row_ids(drafts, rows, source * own_seqs) - shard * width
    capped = SOFT_CAP * jnp.tanh(logits * (1.0 / SOFT_CAP))
    totals = jnp.sum(jnp.exp(capped), axis=1, keepdims=True)
    columns = lax.broadcasted_iota(jnp.int32, (rows, width), 1)
    picks = jnp.sum(jnp.where(columns == ids, capped, 0.0), axis=1, keepdims=True)
    lines = payload_lines(seqs, own_seqs)
    totals = spread(totals, [p * seqs + source * own_seqs for p in range(POSITIONS)], lines)
    picks = spread(picks, [POSITIONS * seqs + p * own_seqs for p in range(DRAFTS)], lines)
    return totals, picks


def parts_for(receiver, source, totals, picks):
    return totals + jnp.where(source == receiver, picks, 0.0)


def half_kernel(hidden_ref, half_ref, done):
    depth = half_ref.shape[1]
    start = pl.multiple_of(lax.rem(lax.axis_index("vocab"), 2) * depth, depth)
    copy = pltpu.make_async_copy(hidden_ref.at[:, pl.ds(start, depth)], half_ref, done)
    copy.start()
    copy.wait()


def own_kernel(hidden_ref, weight_ref, drafts_ref, parts_ref):
    logits = jnp.dot(hidden_ref[...], weight_ref[...], preferred_element_type=jnp.float32)
    me = lax.axis_index("dp")
    totals, picks = contribution(logits, drafts_ref[...], me)
    for receiver in range(parts_ref.shape[0]):
        parts_ref[receiver] = parts_for(receiver, me, totals, picks)


def near_kernel(near_ref, weight_ref, logits_ref):
    depth = near_ref.shape[1]
    start = pl.multiple_of(lax.rem(lax.axis_index("vocab"), 2) * depth, depth)
    logits_ref[...] = jnp.dot(near_ref[...], weight_ref[pl.ds(start, depth), :], preferred_element_type=jnp.float32)


def far_kernel(shift, far_ref, weight_ref, logits_ref, drafts_ref, before_ref, parts_ref):
    depth = far_ref.shape[1]
    dp = before_ref.shape[0]
    copies = parts_ref.shape[0] // dp
    source = lax.rem(lax.axis_index("dp") + dp - shift, dp)
    start = pl.multiple_of((1 - lax.rem(lax.axis_index("vocab"), 2)) * depth, depth)
    logits = logits_ref[...] + jnp.dot(
        far_ref[...], weight_ref[pl.ds(start, depth), :], preferred_element_type=jnp.float32
    )
    totals, picks = contribution(logits, drafts_ref[...], source)
    for receiver in range(dp):
        part = before_ref[receiver] + parts_for(receiver, source, totals, picks)
        parts_ref[receiver * copies : (receiver + 1) * copies] = jnp.broadcast_to(part[None], (copies,) + part.shape)


def gather_rows(flat, starts, count):
    lines = flat.shape[0]
    lane = lax.broadcasted_iota(jnp.int32, (1, LANES), 1)
    out = []
    for low, high, start in starts:
        row = jnp.zeros((1, LANES), jnp.float32)
        for line in range(low // LANES, min(lines, (high - 1) // LANES + 1)):
            place = start - line * LANES
            moved = pltpu.roll(flat, lax.rem(lines * LANES - place, LANES), 1)[line : line + 1]
            row = jnp.where((lane + place >= 0) & (lane + place < LANES), moved, row)
        out.append(row[:, :count])
    return jnp.concatenate(out, axis=0)


def tail_kernel(seqs, parts_ref, cutoffs_ref, norm_ref, logprob_ref, expected_ref, loss_ref):
    own_seqs = cutoffs_ref.shape[1]
    flat = jnp.sum(parts_ref[...], axis=0)
    place = lax.broadcasted_iota(jnp.int32, flat.shape, 0) * LANES + lax.broadcasted_iota(jnp.int32, flat.shape, 1)
    log_total = jnp.log(jnp.where(place < POSITIONS * seqs, flat, 1.0))
    squares = jnp.sum(jnp.sum(log_total * log_total, axis=1, keepdims=True), axis=0, keepdims=True)
    loss_ref[...] = squares * (Z_WEIGHT / (seqs * POSITIONS))
    first = lax.axis_index("dp") * own_seqs
    ranges = [(p * seqs, (p + 1) * seqs, p * seqs + first) for p in range(POSITIONS)]
    log_norm = gather_rows(log_total, ranges, own_seqs)
    base = POSITIONS * seqs
    ranges = [(base + p * own_seqs, base + (p + 1) * own_seqs, base + p * own_seqs) for p in range(DRAFTS)]
    picks = gather_rows(flat, ranges, own_seqs)
    norm_ref[...] = log_norm
    logprob = picks - log_norm[:DRAFTS]
    logprob_ref[...] = logprob
    accept = jax.nn.sigmoid(logprob - cutoffs_ref[...].astype(jnp.float32) / 1024.0)
    product = accept[0:1]
    expected = product
    for p in range(1, DRAFTS):
        product = product * accept[p : p + 1]
        expected = expected + product
    expected_ref[...] = expected


def local(hidden, head_weight, drafts, cutoffs):
    dp, vocab = lax.axis_size("dp"), lax.axis_size("vocab")
    rows, depth = hidden.shape
    width = head_weight.shape[1]
    seqs, own_seqs = drafts.shape[0], rows // POSITIONS
    half = depth // 2
    lines = payload_lines(seqs, own_seqs)
    params = pltpu.CompilerParams(vmem_limit_bytes=GRANT)
    cost = pl.CostEstimate(
        flops=2 * rows * depth * width, bytes_accessed=2 * depth * (rows + width), transcendentals=2 * rows * width
    )
    half_cost = pl.CostEstimate(
        flops=rows * depth * width, bytes_accessed=depth * (rows + width), transcendentals=0
    )
    swap = [(i, i ^ 1) for i in range(vocab)]
    mine = pl.pallas_call(
        half_kernel,
        out_shape=jax.ShapeDtypeStruct((rows, half), hidden.dtype),
        in_specs=[pl.BlockSpec(memory_space=pltpu.HBM)],
        out_specs=VMEM,
        scratch_shapes=[pltpu.SemaphoreType.DMA],
        compiler_params=params,
        name="own_half",
    )(hidden)
    near = [lax.ppermute(mine, "dp", [(i, (i + k) % dp) for i in range(dp)]) for k in range(1, dp)]
    tokens = drafts.T
    parts = pl.pallas_call(
        own_kernel,
        out_shape=jax.ShapeDtypeStruct((dp, lines, LANES), jnp.float32),
        in_specs=[VMEM] * 3,
        out_specs=VMEM,
        cost_estimate=cost,
        compiler_params=params,
        name="own_rows",
    )(hidden, head_weight, tokens)
    near, parts = lax.optimization_barrier((near, parts))
    far = [lax.ppermute(block, "vocab", swap) for block in near]
    for k in range(1, dp):
        count = dp * vocab if k == dp - 1 else dp
        logits = pl.pallas_call(
            near_kernel,
            out_shape=jax.ShapeDtypeStruct((rows, width), jnp.float32),
            in_specs=[VMEM] * 2,
            out_specs=VMEM,
            cost_estimate=half_cost,
            compiler_params=params,
            name="near_half",
        )(near[k - 1], head_weight)
        parts = pl.pallas_call(
            functools.partial(far_kernel, k),
            out_shape=jax.ShapeDtypeStruct((count, lines, LANES), jnp.float32),
            in_specs=[VMEM] * 5,
            out_specs=VMEM,
            cost_estimate=half_cost,
            compiler_params=params,
            name="far_half",
        )(far[k - 1], head_weight, logits, tokens, parts)
    parts = lax.all_to_all(parts, ("dp", "vocab"), 0, 0)
    log_norm, logprob, expected, loss = pl.pallas_call(
        functools.partial(tail_kernel, seqs),
        out_shape=(
            jax.ShapeDtypeStruct((POSITIONS, own_seqs), jnp.float32),
            jax.ShapeDtypeStruct((DRAFTS, own_seqs), jnp.float32),
            jax.ShapeDtypeStruct((1, own_seqs), jnp.float32),
            jax.ShapeDtypeStruct((1, 1), jnp.float32),
        ),
        in_specs=[VMEM] * 2,
        out_specs=(VMEM,) * 4,
        compiler_params=params,
        name="tail",
    )(parts, cutoffs.T)
    return log_norm.T, logprob.T, expected.reshape(own_seqs), loss.reshape(())


def solution(mesh):
    in_specs = (P("dp", None), P(None, ("dp", "vocab")), P(), P("dp", None))
    out_specs = (P("dp", None), P("dp", None), P("dp"), P())
    return jax.shard_map(local, mesh=mesh, in_specs=in_specs, out_specs=out_specs, check_vma=False)
```

time: 31.1 us -> 29.9 us (0.961)
  local copies, waits for them, and re-layouts: 5.16 us -> 4.14 us
  blocking collectives: 14.1 us -> 13.2 us
  waiting for transfers between devices: 5.07 us -> 5.64 us
    ppermute x1, waiting for transfers between devices: 3.39 us -> 4.48 us  [local(): lax.ppermute(mine, 'dp', [(i, (i + k) % dp) for i in range(dp)])]
    dynamic_slice x1 -> x0, local copies, waits for them, and re-layouts: 1.02 us -> none  [local(): mine = lax.dynamic_slice_in_dim(hidden, core * half, half, 1)]
    all_to_all x1, blocking collectives: 14.1 us -> 13.2 us  [local(): parts = lax.all_to_all(parts, ('dp', 'vocab'), 0, 0)]
    ppermute x1, waiting for transfers between devices: 1.68 us -> 1.16 us  [local(): far = [lax.ppermute(block, 'vocab', swap) for block in near]]
    pallas_call x2 -> x4, Pallas kernels: 2.12 us -> 2.3 us  [the longest x1 1.07 us: local(): pl.pallas_call(own_kernel, out_shape=jax.ShapeDtypeStruct((dp, lines, LAN...]
  transfers between devices with their start and end apart: 2 -> 2, of which waited for: 2 -> 2; matrix products, arithmetic and copies ran while one was open for 0% -> 0% of each run, Pallas kernels for 3% -> 5%
where the time goes in v2:
time: 29.9 us; the launch traced here: 29.7 us
  blocking collectives  13.2 us (44%)
  waiting for transfers between devices  5.64 us (19%)
  local copies, waits for them, and re-layouts  4.14 us (14%)
  starting transfers between devices  3.03 us (10%)
  Pallas kernels  3.01 us (10%)
  between operations  0.67 us (2%)
    all_to_all x1, blocking collectives, local(): parts = lax.all_to_all(parts, ('dp', 'vocab'), 0, 0)  13.2 us
    ppermute x1, waiting for transfers between devices, local(): lax.ppermute(mine, 'dp', [(i, (i + k) % dp) for i in range(dp)])  4.48 us
    unnamed x10, local copies, waits for them, and re-layouts  4.14 us
    ppermute x1, starting transfers between devices, local(): lax.ppermute(mine, 'dp', [(i, (i + k) % dp) for i in range(dp)])  3.03 us
    ppermute x1, waiting for transfers between devices, local(): far = [lax.ppermute(block, 'vocab', swap) for block in near]  1.16 us
    pallas_call x1, Pallas kernels, local(): pl.pallas_call(own_kernel, out_shape=jax.ShapeDtypeStruct((dp, lines, LAN...  1.07 us
    pallas_call x1, Pallas kernels, local(): pl.pallas_call(functools.partial(tail_kernel, seqs), out_shape=(jax.Shape...  0.71 us
    pallas_call x1, Pallas kernels, local(): pl.pallas_call(functools.partial(far_kernel, k), out_shape=jax.ShapeDtype...  0.68 us
  transfers between devices with their start and end apart: 2, of which 2 were waited for; matrix products, arithmetic and copies ran while one was open for 0% of the time, Pallas kernels for 5%

profile of v2, /device:TPU:0, one launch (start us, length us, event | category | flops | bytes accessed | tf_op | source)
XLA Modules:
  0.0 29.7 jit_solution(13933282580110113278)
XLA Ops:
  0.6 0.0 copy-start.2
  0.6 1.1 %copy-done.2 = bf16[80,4608]{1,0:T(8,128)(2,1)S(1)} copy-done((bf16[80,4608]{1,0:T(8,128)(2,1)S(1)}, bf16[80,4608]{1,0:T(8,128)(2,1)}, u32[]{:S(2)}) %copy-start.2) | copy-done | bytes 737304
  1.8 3.0 %collective-permute-start = (bf16[80,2304]{1,0:T(8,128)(2,1)S(1)}, bf16[80,2304]{1,0:T(8,128)(2,1)S(1)}, u32[]{:S(2)}, u32[]{:S(2)}) collective-permute-start(bf16[80,2304]{1,0:T(8,128)(2,1)S(1)} %own_half.1), channel_id=1, source_target_pairs={{0,16},{16,0},{1,17},{17,1},{2,18},{18,2},{3,19},{19,3},{4,20},{20... | collective-permute-start | bytes 1105928 | tf_op jit(solution)/shard_map/ppermute | solution.py:165
  4.8 0.0 copy-start
  4.8 2.3 %copy-done = bf16[4608,512]{1,0:T(8,128)(2,1)S(1)} copy-done((bf16[4608,512]{1,0:T(8,128)(2,1)S(1)}, bf16[4608,512]{1,0:T(8,128)(2,1)}, u32[]{:S(2)}) %copy-start) | copy-done | bytes 4718616
  7.2 0.0 copy-start.3
  7.2 0.7 %copy-done.3 = s32[32,4]{0,1:T(4,128)S(1)} copy-done((s32[32,4]{0,1:T(4,128)S(1)}, s32[32,4]{0,1:T(4,128)}, u32[]{:S(2)}) %copy-start.3) | copy-done | bytes 536
  7.8 0.0 copy-start.1
  7.8 1.1 %own_rows.1.before_ref = f32[2,2,128]{2,1,0:T(2,128)S(1)} custom-call(bf16[80,4608]{1,0:T(8,128)(2,1)S(1)} %copy-done.2, bf16[4608,512]{1,0:T(8,128)(2,1)S(1)} %copy-done, s32[4,32]{1,0:T(4,128)S(1)} %bitcast.6), custom_call_target="tpu_custom_call" | custom-call | flops 377487360 | bytes 5455872 | tf_op jit(solution)/shard_map/own_rows/pallas_call | solution.py:167
  8.9 0.0 copy-start.4
  8.9 4.5 %collective-permute-done.near_ref = bf16[80,2304]{1,0:T(8,128)(2,1)S(1)} collective-permute-done((bf16[80,2304]{1,0:T(8,128)(2,1)S(1)}, bf16[80,2304]{1,0:T(8,128)(2,1)S(1)}, u32[]{:S(2)}, u32[]{:S(2)}) %collective-permute-start) | collective-permute-done | bytes 368672 | tf_op jit(solution)/shard_map/ppermute | solution.py:165
  13.4 0.0 collective-permute-start.1
  13.4 0.0 copy-done.1
  13.4 0.5 %near_half.1.logits_ref = f32[80,512]{1,0:T(8,128)S(1)} custom-call(bf16[80,2304]{1,0:T(8,128)(2,1)S(1)} %collective-permute-done.near_ref, bf16[4608,512]{1,0:T(8,128)(2,1)S(1)} %copy-done.1), custom_call_target="tpu_custom_call" | custom-call | flops 188743680 | bytes 2727936 | tf_op jit(solution)/shard_map/near_half/pallas_call | solution.py:180
  13.9 1.2 %collective-permute-done.1.far_ref = bf16[80,2304]{1,0:T(8,128)(2,1)S(1)} collective-permute-done((bf16[80,2304]{1,0:T(8,128)(2,1)S(1)}, bf16[80,2304]{1,0:T(8,128)(2,1)S(1)}, u32[]{:S(2)}, u32[]{:S(2)}) %collective-permute-start.1) | collective-permute-done | bytes 368672 | tf_op jit(solution)/shard_map/ppermute | solution.py:177
  15.1 0.7 %far_half.1 = f32[32,2,128]{2,1,0:T(2,128)S(1)} custom-call(bf16[80,2304]{1,0:T(8,128)(2,1)S(1)} %collective-permute-done.1.far_ref, bf16[4608,512]{1,0:T(8,128)(2,1)S(1)} %copy-done.1, f32[80,512]{1,0:T(8,128)S(1)} %near_half.1.logits_ref, s32[4,32]{1,0:T(4,128)S(1)} %bitcast.7, f32[2,2,128]{2,1,0:T(2,128)S(1)} %own_rows.1.before_ref), custom_call_target="tpu_custom_call" | custom-call | flops 188743680 | bytes 2727936 | tf_op jit(solution)/shard_map/far_half/pallas_call | solution.py:189
  15.8 13.2 %all_to_all.5.parts_ref = f32[32,2,128]{2,1,0:T(2,128)S(1)} all-to-all(f32[32,2,128]{2,1,0:T(2,128)S(1)} %far_half.1), channel_id=1, replica_groups=mesh['dp'=2,'vocab'=16] {'dp','vocab'}, dimensions={0} | all-to-all | bytes 65536 | tf_op jit(solution)/shard_map/all_to_all | solution.py:198
  28.9 0.0 copy-done.4
  29.0 0.7 %tail.1 = (f32[5,16]{1,0:T(8,128)}, f32[4,16]{1,0:T(4,128)}, f32[1,16]{1,0:T(1,128)}, f32[1,1]{1,0:T(1,128)}) custom-call(f32[32,2,128]{2,1,0:T(2,128)S(1)} %all_to_all.5.parts_ref, s32[4,16]{1,0:T(4,128)S(1)} %bitcast.8), custom_call_target="tpu_custom_call" | custom-call | tf_op jit(solution)/shard_map/tail/pallas_call | solution.py:199
  (1 shorter events, 0.0 us)
Async XLA Ops:
  0.6 1.1 %copy-start.2 = (bf16[80,4608]{1,0:T(8,128)(2,1)S(1)}, bf16[80,4608]{1,0:T(8,128)(2,1)}, u32[]{:S(2)}) copy-start(bf16[80,4608]{1,0:T(8,128)(2,1)} %hidden_ref.3) | copy-start | bytes 2211844
  1.8 11.6 %collective-permute-start = (bf16[80,2304]{1,0:T(8,128)(2,1)S(1)}, bf16[80,2304]{1,0:T(8,128)(2,1)S(1)}, u32[]{:S(2)}, u32[]{:S(2)}) collective-permute-start(bf16[80,2304]{1,0:T(8,128)(2,1)S(1)} %own_half.1), channel_id=1, source_target_pairs={{0,16},{16,0},{1,17},{17,1},{2,18},{18,2},{3,19},{19,3},{4,20},{20... | collective-permute-start | bytes 1105928 | tf_op jit(solution)/shard_map/ppermute | solution.py:165
  4.8 2.3 %copy-start = (bf16[4608,512]{1,0:T(8,128)(2,1)S(1)}, bf16[4608,512]{1,0:T(8,128)(2,1)}, u32[]{:S(2)}) copy-start(bf16[4608,512]{1,0:T(8,128)(2,1)} %weight_ref.5) | copy-start | bytes 14155780
  7.2 0.7 %copy-start.3 = (s32[32,4]{0,1:T(4,128)S(1)}, s32[32,4]{0,1:T(4,128)}, u32[]{:S(2)}) copy-start(s32[32,4]{0,1:T(4,128)} %param.6) | copy-start | bytes 1540
  7.8 5.6 %copy-start.1 = (bf16[4608,512]{1,0:T(8,128)(2,1)S(1)}, bf16[4608,512]{1,0:T(8,128)(2,1)}, u32[]{:S(2)}) copy-start(bf16[4608,512]{1,0:T(8,128)(2,1)} %weight_ref.5) | copy-start | bytes 14155780
  8.9 20.0 %copy-start.4 = (s32[16,4]{0,1:T(4,128)S(1)}, s32[16,4]{0,1:T(4,128)}, u32[]{:S(2)}) copy-start(s32[16,4]{0,1:T(4,128)} %param.7) | copy-start | bytes 772
  13.4 1.7 %collective-permute-start.1 = (bf16[80,2304]{1,0:T(8,128)(2,1)S(1)}, bf16[80,2304]{1,0:T(8,128)(2,1)S(1)}, u32[]{:S(2)}, u32[]{:S(2)}) collective-permute-start(bf16[80,2304]{1,0:T(8,128)(2,1)S(1)} %collective-permute-done.near_ref), channel_id=1, source_target_pairs={{0,1},{1,0},{2,3},{3,2},{4,5},{5,4},{6,7},{7,6},{8,9},{9,8},{10,11... | collective-permute-start | bytes 1105928 | tf_op jit(solution)/shard_map/ppermute | solution.py:177

commit v3 on v2

--- a/solution.py
+++ b/solution.py
@@ -7,12 +7,15 @@
 from jax.experimental.pallas import tpu as pltpu
 from jax.sharding import PartitionSpec as P
 
+
 DRAFTS = 4
 POSITIONS = 5
 SOFT_CAP = 30.0
 Z_WEIGHT = 0.001
 LANES = 128
 GRANT = 16 * 2**20
+RELAYED = 3 * LANES
+CHUNKS = 9
 VMEM = pl.BlockSpec(memory_space=pltpu.VMEM)
 
 
@@ -62,37 +65,56 @@
     return totals + jnp.where(source == receiver, picks, 0.0)
 
 
-def half_kernel(hidden_ref, half_ref, done):
-    depth = half_ref.shape[1]
-    start = pl.multiple_of(lax.rem(lax.axis_index("vocab"), 2) * depth, depth)
-    copy = pltpu.make_async_copy(hidden_ref.at[:, pl.ds(start, depth)], half_ref, done)
-    copy.start()
-    copy.wait()
-
-
-def own_kernel(hidden_ref, weight_ref, drafts_ref, parts_ref):
-    logits = jnp.dot(hidden_ref[...], weight_ref[...], preferred_element_type=jnp.float32)
+def place(size, piece, other_row, other_core):
+    me = lax.axis_index("vocab")
+    core = lax.rem(me + other_core, 2)
+    row = lax.rem(me // 2 + other_row, 2)
+    return pl.multiple_of((4 * RELAYED + core * size) if piece else (2 * row + core) * size, LANES)
+
+
+def pieces_kernel(hidden_ref, *piece_refs):
+    for piece, ref in enumerate(piece_refs):
+        size = ref.shape[1]
+        ref[...] = hidden_ref[:, pl.ds(place(size, piece, 0, 0), size)]
+
+
+def product(rows_ref, weight_ref, piece, other_row, other_core):
+    size = rows_ref.shape[1]
+    block = weight_ref[pl.ds(place(size, piece, other_row, other_core), size), :]
+    return jnp.dot(rows_ref[...], block, preferred_element_type=jnp.float32)
+
+
+def own_kernel(hidden_ref, weight_ref, drafts_ref, parts_ref, held_ref, tokens_ref, arrived, drafts_arrived):
+    depth = weight_ref.shape[0]
+    step = depth // CHUNKS
+    blocks = [pl.ds(i * step, step) for i in range(CHUNKS)]
+    copies = [pltpu.make_async_copy(weight_ref.at[b], held_ref.at[b], arrived.at[i]) for i, b in enumerate(blocks)]
+    tokens = pltpu.make_async_copy(drafts_ref, tokens_ref, drafts_arrived)
+    for copy in copies:
+        copy.start()
+    tokens.start()
+    logits = jnp.zeros((hidden_ref.shape[0], weight_ref.shape[1]), jnp.float32)
+    for block, copy in zip(blocks, copies):
+        copy.wait()
+        logits += jnp.dot(hidden_ref[:, block], held_ref[block, :], preferred_element_type=jnp.float32)
+    tokens.wait()
     me = lax.axis_index("dp")
-    totals, picks = contribution(logits, drafts_ref[...], me)
+    totals, picks = contribution(logits, tokens_ref[...], me)
     for receiver in range(parts_ref.shape[0]):
         parts_ref[receiver] = parts_for(receiver, me, totals, picks)
 
 
-def near_kernel(near_ref, weight_ref, logits_ref):
-    depth = near_ref.shape[1]
-    start = pl.multiple_of(lax.rem(lax.axis_index("vocab"), 2) * depth, depth)
-    logits_ref[...] = jnp.dot(near_ref[...], weight_ref[pl.ds(start, depth), :], preferred_element_type=jnp.float32)
-
-
-def far_kernel(shift, far_ref, weight_ref, logits_ref, drafts_ref, before_ref, parts_ref):
-    depth = far_ref.shape[1]
+def near_kernel(first_ref, swapped_ref, relayed_ref, second_ref, weight_ref, logits_ref):
+    logits = product(first_ref, weight_ref, 0, 0, 0) + product(swapped_ref, weight_ref, 0, 0, 1)
+    logits += product(relayed_ref, weight_ref, 0, 1, 0)
+    logits_ref[...] = logits + product(second_ref, weight_ref, 1, 0, 0)
+
+
+def far_kernel(shift, relayed_ref, second_ref, weight_ref, logits_ref, drafts_ref, before_ref, parts_ref):
     dp = before_ref.shape[0]
     copies = parts_ref.shape[0] // dp
     source = lax.rem(lax.axis_index("dp") + dp - shift, dp)
-    start = pl.multiple_of((1 - lax.rem(lax.axis_index("vocab"), 2)) * depth, depth)
-    logits = logits_ref[...] + jnp.dot(
-        far_ref[...], weight_ref[pl.ds(start, depth), :], preferred_element_type=jnp.float32
-    )
+    logits = logits_ref[...] + product(relayed_ref, weight_ref, 0, 1, 1) + product(second_ref, weight_ref, 1, 0, 1)
     totals, picks = contribution(logits, drafts_ref[...], source)
     for receiver in range(dp):
         part = before_ref[receiver] + parts_for(receiver, source, totals, picks)
@@ -143,7 +165,7 @@
     rows, depth = hidden.shape
     width = head_weight.shape[1]
     seqs, own_seqs = drafts.shape[0], rows // POSITIONS
-    half = depth // 2
+    second = depth // 2 - 2 * RELAYED
     lines = payload_lines(seqs, own_seqs)
     params = pltpu.CompilerParams(vmem_limit_bytes=GRANT)
     cost = pl.CostEstimate(
@@ -153,48 +175,64 @@
         flops=rows * depth * width, bytes_accessed=depth * (rows + width), transcendentals=0
     )
     swap = [(i, i ^ 1) for i in range(vocab)]
-    mine = pl.pallas_call(
-        half_kernel,
-        out_shape=jax.ShapeDtypeStruct((rows, half), hidden.dtype),
-        in_specs=[pl.BlockSpec(memory_space=pltpu.HBM)],
-        out_specs=VMEM,
-        scratch_shapes=[pltpu.SemaphoreType.DMA],
+    relay = [(i, i ^ 2) for i in range(vocab)]
+    pieces = pl.pallas_call(
+        pieces_kernel,
+        out_shape=[jax.ShapeDtypeStruct((rows, size), hidden.dtype) for size in (RELAYED, second)],
+        in_specs=[VMEM],
+        out_specs=[VMEM] * 2,
         compiler_params=params,
-        name="own_half",
+        name="pieces",
     )(hidden)
-    near = [lax.ppermute(mine, "dp", [(i, (i + k) % dp) for i in range(dp)]) for k in range(1, dp)]
-    tokens = drafts.T
-    parts = pl.pallas_call(
+    others = []
+    for k in range(1, dp):
+        shift = [(i, (i + k) % dp) for i in range(dp)]
+        first = lax.ppermute(pieces[0], "dp", shift)
+        both = lax.ppermute(pieces[1], "dp", shift)
+        relayed = lax.ppermute(first, "vocab", relay)
+        others.append((first, both, relayed, lax.ppermute(first, "vocab", swap)))
+    parts, held, tokens = pl.pallas_call(
         own_kernel,
-        out_shape=jax.ShapeDtypeStruct((dp, lines, LANES), jnp.float32),
-        in_specs=[VMEM] * 3,
-        out_specs=VMEM,
+        out_shape=(
+            jax.ShapeDtypeStruct((dp, lines, LANES), jnp.float32),
+            pltpu.VMEM(head_weight.shape, head_weight.dtype),
+            pltpu.VMEM((DRAFTS, seqs), drafts.dtype),
+        ),
+        in_specs=[VMEM, pl.BlockSpec(memory_space=pl.ANY), pl.BlockSpec(memory_space=pl.ANY)],
+        out_specs=(VMEM,) * 3,
+        scratch_shapes=[pltpu.SemaphoreType.DMA((CHUNKS,)), pltpu.SemaphoreType.DMA],
         cost_estimate=cost,
         compiler_params=params,
         name="own_rows",
-    )(hidden, head_weight, tokens)
-    near, parts = lax.optimization_barrier((near, parts))
-    far = [lax.ppermute(block, "vocab", swap) for block in near]
+    )(
+        hidden,
+        pltpu.with_memory_space_constraint(head_weight, pltpu.HBM),
+        pltpu.with_memory_space_constraint(drafts.T, pltpu.HBM),
+    )
     for k in range(1, dp):
+        first, both, relayed, first_swapped = others[k - 1]
+        both, relayed, first_swapped = lax.optimization_barrier((both, relayed, first_swapped))
+        relayed_swapped = lax.ppermute(relayed, "vocab", swap)
+        both_swapped = lax.ppermute(both, "vocab", swap)
         count = dp * vocab if k == dp - 1 else dp
         logits = pl.pallas_call(
             near_kernel,
             out_shape=jax.ShapeDtypeStruct((rows, width), jnp.float32),
-            in_specs=[VMEM] * 2,
-            out_specs=VMEM,
-            cost_estimate=half_cost,
-            compiler_params=params,
-            name="near_half",
-        )(near[k - 1], head_weight)
-        parts = pl.pallas_call(
-            functools.partial(far_kernel, k),
-            out_shape=jax.ShapeDtypeStruct((count, lines, LANES), jnp.float32),
             in_specs=[VMEM] * 5,
             out_specs=VMEM,
             cost_estimate=half_cost,
             compiler_params=params,
-            name="far_half",
-        )(far[k - 1], head_weight, logits, tokens, parts)
+            name="near",
+        )(first, first_swapped, relayed, both, held)
+        parts = pl.pallas_call(
+            functools.partial(far_kernel, k),
+            out_shape=jax.ShapeDtypeStruct((count, lines, LANES), jnp.float32),
+            in_specs=[VMEM] * 6,
+            out_specs=VMEM,
+            cost_estimate=half_cost,
+            compiler_params=params,
+            name="far",
+        )(relayed_swapped, both_swapped, held, logits, tokens, parts)
     parts = lax.all_to_all(parts, ("dp", "vocab"), 0, 0)
     log_norm, logprob, expected, loss = pl.pallas_call(
         functools.partial(tail_kernel, seqs),

time: 29.9 us -> 35 us (1.17)
  waiting for transfers between devices: 5.64 us -> 9.65 us
  local copies, waits for them, and re-layouts: 4.14 us -> 1.12 us
  starting transfers between devices: 3.03 us -> 5.39 us
  Pallas kernels: 3.01 us -> 4.81 us
    ppermute x2 -> x6, waiting for transfers between devices: 5.64 us -> 9.65 us  [the longest x1 7.19 us: local(): first = lax.ppermute(pieces[0], 'dp', shift)]
    unnamed x10 -> x4, local copies, waits for them, and re-layouts: 4.14 us -> 1.12 us
    ppermute x2 -> x6, starting transfers between devices: 3.03 us -> 5.39 us  [the longest x1 3.03 us: local(): both = lax.ppermute(pieces[1], 'dp', shift)]
    pallas_call x2, Pallas kernels: 1.1 us -> 2.84 us  [the longest x1 2.82 us: local(): pl.pallas_call(own_kernel, out_shape=(jax.ShapeDtypeStruct((dp, lines, LA...]
  transfers between devices with their start and end apart: 2 -> 6, of which waited for: 2 -> 2; matrix products, arithmetic and copies ran while one was open for 0% -> 0% of each run, Pallas kernels for 5% -> 10%
where the time goes in v3:
time: 35 us; the launch traced here: 34.8 us
  blocking collectives  13.2 us (38%)
  waiting for transfers between devices  9.65 us (28%)
  starting transfers between devices  5.39 us (15%)
  Pallas kernels  4.81 us (14%)
  local copies, waits for them, and re-layouts  1.12 us (3%)
  between operations  0.7 us (2%)
    all_to_all x1, blocking collectives, local(): parts = lax.all_to_all(parts, ('dp', 'vocab'), 0, 0)  13.2 us
    ppermute x1, waiting for transfers between devices, local(): first = lax.ppermute(pieces[0], 'dp', shift)  7.19 us
    ppermute x1, starting transfers between devices, local(): both = lax.ppermute(pieces[1], 'dp', shift)  3.03 us
    pallas_call x1, Pallas kernels, local(): pl.pallas_call(own_kernel, out_shape=(jax.ShapeDtypeStruct((dp, lines, LA...  2.82 us
    ppermute x1, waiting for transfers between devices, local(): relayed = lax.ppermute(first, 'vocab', relay)  2.45 us
    ppermute x1, starting transfers between devices, local(): relayed = lax.ppermute(first, 'vocab', relay)  1.77 us
    unnamed x4, local copies, waits for them, and re-layouts  1.12 us
    pallas_call x1, Pallas kernels, local(): pl.pallas_call(functools.partial(tail_kernel, seqs), out_shape=(jax.Shape...  0.71 us
  transfers between devices with their start and end apart: 6, of which 2 were waited for; matrix products, arithmetic and copies ran while one was open for 0% of the time, Pallas kernels for 10%

profile of v3, /device:TPU:0, one launch (start us, length us, event | category | flops | bytes accessed | tf_op | source)
XLA Modules:
  0.0 34.8 jit_solution(9847875373930777230)
XLA Ops:
  0.6 0.0 copy-start
  0.6 1.1 %copy-done = bf16[80,4608]{1,0:T(8,128)(2,1)S(1)} copy-done((bf16[80,4608]{1,0:T(8,128)(2,1)S(1)}, bf16[80,4608]{1,0:T(8,128)(2,1)}, u32[]{:S(2)}) %copy-start) | copy-done | bytes 737304
  1.8 3.0 %collective-permute-start = (bf16[80,1536]{1,0:T(8,128)(2,1)S(1)}, bf16[80,1536]{1,0:T(8,128)(2,1)S(1)}, u32[]{:S(2)}, u32[]{:S(2)}) collective-permute-start(bf16[80,1536]{1,0:T(8,128)(2,1)S(1)} %get-tuple-element.16), channel_id=1, source_target_pairs={{0,16},{16,0},{1,17},{17,1},{2,18},{18,2},{3,19},{19,3},{4,20},{20... | collective-permute-start | bytes 737288 | tf_op jit(solution)/shard_map/ppermute | solution.py:191
  4.8 0.1 collective-permute-start.1
  4.9 7.2 %collective-permute-done.1.first_ref = bf16[80,384]{1,0:T(8,128)(2,1)S(1)} collective-permute-done((bf16[80,384]{1,0:T(8,128)(2,1)S(1)}, bf16[80,384]{1,0:T(8,128)(2,1)S(1)}, u32[]{:S(2)}, u32[]{:S(2)}) %collective-permute-start.1) | collective-permute-done | bytes 61472 | tf_op jit(solution)/shard_map/ppermute | solution.py:190
  12.1 1.8 %collective-permute-start.2 = (bf16[80,384]{1,0:T(8,128)(2,1)S(1)}, bf16[80,384]{1,0:T(8,128)(2,1)S(1)}, u32[]{:S(2)}, u32[]{:S(2)}) collective-permute-start(bf16[80,384]{1,0:T(8,128)(2,1)S(1)} %collective-permute-done.1.first_ref), channel_id=1, source_target_pairs={{0,2},{1,3},{2,0},{3,1},{4,6},{5,7},{6,4},{7,5},{8,10},{9,11},{10,... | collective-permute-start | bytes 184328 | tf_op jit(solution)/shard_map/ppermute | solution.py:192
  13.8 0.0 collective-permute-start.3
  13.8 2.4 %collective-permute-done.2.relayed_ref = bf16[80,384]{1,0:T(8,128)(2,1)S(1)} collective-permute-done((bf16[80,384]{1,0:T(8,128)(2,1)S(1)}, bf16[80,384]{1,0:T(8,128)(2,1)S(1)}, u32[]{:S(2)}, u32[]{:S(2)}) %collective-permute-start.2) | collective-permute-done | bytes 61472 | tf_op jit(solution)/shard_map/ppermute | solution.py:192
  16.3 0.0 collective-permute-done.3.swapped_ref
  16.3 0.0 collective-permute-done.second_ref
  16.3 0.0 collective-permute-start.5
  16.3 0.5 %collective-permute-start.4 = (bf16[80,384]{1,0:T(8,128)(2,1)S(1)}, bf16[80,384]{1,0:T(8,128)(2,1)S(1)}, u32[]{:S(2)}, u32[]{:S(2)}) collective-permute-start(bf16[80,384]{1,0:T(8,128)(2,1)S(1)} %collective-permute-done.2.relayed_ref), channel_id=1, source_target_pairs={{0,1},{1,0},{2,3},{3,2},{4,5},{5,4},{6,7},{7,6},{8,9},{9,8},{10,11... | collective-permute-start | bytes 184328 | tf_op jit(solution)/shard_map/ppermute | solution.py:215
  16.8 2.8 %own_rows.1 = (f32[2,2,128]{2,1,0:T(2,128)S(1)}, bf16[4608,512]{1,0:T(8,128)(2,1)S(1)}, s32[4,32]{1,0:T(4,128)S(1)}) custom-call(bf16[80,4608]{1,0:T(8,128)(2,1)S(1)} %copy-done, bf16[4608,512]{1,0:T(8,128)(2,1)} %weight_ref.1, s32[4,32]{1,0:T(4,128)} %bitcast.7), custom_call_target="tpu_custom_call" | custom-call | flops 377487360 | bytes 5455872 | tf_op jit(solution)/shard_map/own_rows/pallas_call | solution.py:194
  19.6 0.0 copy-start.1
  19.7 0.6 %near.1.logits_ref = f32[80,512]{1,0:T(8,128)S(1)} custom-call(bf16[80,384]{1,0:T(8,128)(2,1)S(1)} %collective-permute-done.1.first_ref, bf16[80,384]{1,0:T(8,128)(2,1)S(1)} %collective-permute-done.3.swapped_ref, bf16[80,384]{1,0:T(8,128)(2,1)S(1)} %collective-permute-done.2.relayed_ref, bf16[80,1536]{1,0:T(8,128)(2,1)S(1)} %collective-permute-done.second_ref, ...), custom_call_target="tpu_custom_call" | custom-call | flops 188743680 | bytes 2727936 | tf_op jit(solution)/shard_map/near/pallas_call | solution.py:218
  20.3 0.0 collective-permute-done.4.relayed_ref
  20.3 0.0 collective-permute-done.5.second_ref
  20.3 0.6 %far.1 = f32[32,2,128]{2,1,0:T(2,128)S(1)} custom-call(bf16[80,384]{1,0:T(8,128)(2,1)S(1)} %collective-permute-done.4.relayed_ref, bf16[80,1536]{1,0:T(8,128)(2,1)S(1)} %collective-permute-done.5.second_ref, bf16[4608,512]{1,0:T(8,128)(2,1)S(1)} %get-tuple-element.20.weight_ref, f32[80,512]{1,0:T(8,128)S(1)} %near.1.logits_ref, ...), custom_call_target="tpu_custom_call" | custom-call | flops 188743680 | bytes 2727936 | tf_op jit(solution)/shard_map/far/pallas_call | solution.py:227
  20.9 13.2 %all_to_all.5.parts_ref = f32[32,2,128]{2,1,0:T(2,128)S(1)} all-to-all(f32[32,2,128]{2,1,0:T(2,128)S(1)} %far.1), channel_id=1, replica_groups=mesh['dp'=2,'vocab'=16] {'dp','vocab'}, dimensions={0} | all-to-all | bytes 65536 | tf_op jit(solution)/shard_map/all_to_all | solution.py:236
  34.1 0.0 copy-done.1
  34.1 0.7 %tail.1 = (f32[5,16]{1,0:T(8,128)}, f32[4,16]{1,0:T(4,128)}, f32[1,16]{1,0:T(1,128)}, f32[1,1]{1,0:T(1,128)}) custom-call(f32[32,2,128]{2,1,0:T(2,128)S(1)} %all_to_all.5.parts_ref, s32[4,16]{1,0:T(4,128)S(1)} %bitcast.6), custom_call_target="tpu_custom_call" | custom-call | tf_op jit(solution)/shard_map/tail/pallas_call | solution.py:237
  (1 shorter events, 0.0 us)
Async XLA Ops:
  0.6 1.1 %copy-start = (bf16[80,4608]{1,0:T(8,128)(2,1)S(1)}, bf16[80,4608]{1,0:T(8,128)(2,1)}, u32[]{:S(2)}) copy-start(bf16[80,4608]{1,0:T(8,128)(2,1)} %hidden_ref.3) | copy-start | bytes 2211844
  1.8 14.5 %collective-permute-start = (bf16[80,1536]{1,0:T(8,128)(2,1)S(1)}, bf16[80,1536]{1,0:T(8,128)(2,1)S(1)}, u32[]{:S(2)}, u32[]{:S(2)}) collective-permute-start(bf16[80,1536]{1,0:T(8,128)(2,1)S(1)} %get-tuple-element.16), channel_id=1, source_target_pairs={{0,16},{16,0},{1,17},{17,1},{2,18},{18,2},{3,19},{19,3},{4,20},{20... | collective-permute-start | bytes 737288 | tf_op jit(solution)/shard_map/ppermute | solution.py:191
  4.8 7.3 %collective-permute-start.1 = (bf16[80,384]{1,0:T(8,128)(2,1)S(1)}, bf16[80,384]{1,0:T(8,128)(2,1)S(1)}, u32[]{:S(2)}, u32[]{:S(2)}) collective-permute-start(bf16[80,384]{1,0:T(8,128)(2,1)S(1)} %get-tuple-element.17), channel_id=1, source_target_pairs={{0,16},{16,0},{1,17},{17,1},{2,18},{18,2},{3,19},{19,3},{4,20},{20... | collective-permute-start | bytes 184328 | tf_op jit(solution)/shard_map/ppermute | solution.py:190
  12.1 4.2 %collective-permute-start.2 = (bf16[80,384]{1,0:T(8,128)(2,1)S(1)}, bf16[80,384]{1,0:T(8,128)(2,1)S(1)}, u32[]{:S(2)}, u32[]{:S(2)}) collective-permute-start(bf16[80,384]{1,0:T(8,128)(2,1)S(1)} %collective-permute-done.1.first_ref), channel_id=1, source_target_pairs={{0,2},{1,3},{2,0},{3,1},{4,6},{5,7},{6,4},{7,5},{8,10},{9,11},{10,... | collective-permute-start | bytes 184328 | tf_op jit(solution)/shard_map/ppermute | solution.py:192
  13.8 2.5 %collective-permute-start.3 = (bf16[80,384]{1,0:T(8,128)(2,1)S(1)}, bf16[80,384]{1,0:T(8,128)(2,1)S(1)}, u32[]{:S(2)}, u32[]{:S(2)}) collective-permute-start(bf16[80,384]{1,0:T(8,128)(2,1)S(1)} %collective-permute-done.1.first_ref), channel_id=1, source_target_pairs={{0,1},{1,0},{2,3},{3,2},{4,5},{5,4},{6,7},{7,6},{8,9},{9,8},{10,11... | collective-permute-start | bytes 184328 | tf_op jit(solution)/shard_map/ppermute | solution.py:193
  16.3 4.0 %collective-permute-start.5 = (bf16[80,1536]{1,0:T(8,128)(2,1)S(1)}, bf16[80,1536]{1,0:T(8,128)(2,1)S(1)}, u32[]{:S(2)}, u32[]{:S(2)}) collective-permute-start(bf16[80,1536]{1,0:T(8,128)(2,1)S(1)} %collective-permute-done.second_ref), channel_id=1, source_target_pairs={{0,1},{1,0},{2,3},{3,2},{4,5},{5,4},{6,7},{7,6},{8,9},{9,8},{10,11... | collective-permute-start | bytes 737288 | tf_op jit(solution)/shard_map/ppermute | solution.py:216
  16.3 4.0 %collective-permute-start.4 = (bf16[80,384]{1,0:T(8,128)(2,1)S(1)}, bf16[80,384]{1,0:T(8,128)(2,1)S(1)}, u32[]{:S(2)}, u32[]{:S(2)}) collective-permute-start(bf16[80,384]{1,0:T(8,128)(2,1)S(1)} %collective-permute-done.2.relayed_ref), channel_id=1, source_target_pairs={{0,1},{1,0},{2,3},{3,2},{4,5},{5,4},{6,7},{7,6},{8,9},{9,8},{10,11... | collective-permute-start | bytes 184328 | tf_op jit(solution)/shard_map/ppermute | solution.py:215
  19.6 14.5 %copy-start.1 = (s32[16,4]{0,1:T(4,128)S(1)}, s32[16,4]{0,1:T(4,128)}, u32[]{:S(2)}) copy-start(s32[16,4]{0,1:T(4,128)} %param.7) | copy-start | bytes 772

commit v4 on v3

--- a/solution.py
+++ b/solution.py
@@ -15,8 +15,10 @@
 LANES = 128
 GRANT = 16 * 2**20
 RELAYED = 3 * LANES
-CHUNKS = 9
+EARLY = 8 * LANES
+WEIGHT_HINT = 3_000_000_000
 VMEM = pl.BlockSpec(memory_space=pltpu.VMEM)
+ANY = pl.BlockSpec(memory_space=pl.ANY)
 
 
 def row_ids(drafts, rows, first_seq):
@@ -69,7 +71,8 @@
     me = lax.axis_index("vocab")
     core = lax.rem(me + other_core, 2)
     row = lax.rem(me // 2 + other_row, 2)
-    return pl.multiple_of((4 * RELAYED + core * size) if piece else (2 * row + core) * size, LANES)
+    base = (2 * row * RELAYED, 4 * RELAYED, 4 * RELAYED + 2 * EARLY)[piece]
+    return pl.multiple_of(base + core * size, LANES)
 
 
 def pieces_kernel(hidden_ref, *piece_refs):
@@ -84,37 +87,36 @@
     return jnp.dot(rows_ref[...], block, preferred_element_type=jnp.float32)
 
 
-def own_kernel(hidden_ref, weight_ref, drafts_ref, parts_ref, held_ref, tokens_ref, arrived, drafts_arrived):
-    depth = weight_ref.shape[0]
-    step = depth // CHUNKS
-    blocks = [pl.ds(i * step, step) for i in range(CHUNKS)]
-    copies = [pltpu.make_async_copy(weight_ref.at[b], held_ref.at[b], arrived.at[i]) for i, b in enumerate(blocks)]
-    tokens = pltpu.make_async_copy(drafts_ref, tokens_ref, drafts_arrived)
-    for copy in copies:
-        copy.start()
-    tokens.start()
-    logits = jnp.zeros((hidden_ref.shape[0], weight_ref.shape[1]), jnp.float32)
-    for block, copy in zip(blocks, copies):
-        copy.wait()
-        logits += jnp.dot(hidden_ref[:, block], held_ref[block, :], preferred_element_type=jnp.float32)
-    tokens.wait()
+def tokens_kernel(drafts_ref, tokens_ref, arrived):
+    copy = pltpu.make_async_copy(drafts_ref, tokens_ref, arrived)
+    copy.start()
+    copy.wait()
+
+
+def own_kernel(hidden_ref, weight_ref, tokens_ref, parts_ref):
+    logits = jnp.dot(hidden_ref[...], weight_ref[...], preferred_element_type=jnp.float32)
     me = lax.axis_index("dp")
     totals, picks = contribution(logits, tokens_ref[...], me)
     for receiver in range(parts_ref.shape[0]):
         parts_ref[receiver] = parts_for(receiver, me, totals, picks)
 
 
-def near_kernel(first_ref, swapped_ref, relayed_ref, second_ref, weight_ref, logits_ref):
+def near_kernel(first_ref, swapped_ref, early_ref, weight_ref, logits_ref):
     logits = product(first_ref, weight_ref, 0, 0, 0) + product(swapped_ref, weight_ref, 0, 0, 1)
+    logits_ref[...] = logits + product(early_ref, weight_ref, 1, 0, 0)
+
+
+def middle_kernel(swapped_ref, relayed_ref, late_ref, weight_ref, before_ref, logits_ref):
+    logits = before_ref[...] + product(swapped_ref, weight_ref, 1, 0, 1)
     logits += product(relayed_ref, weight_ref, 0, 1, 0)
-    logits_ref[...] = logits + product(second_ref, weight_ref, 1, 0, 0)
-
-
-def far_kernel(shift, relayed_ref, second_ref, weight_ref, logits_ref, drafts_ref, before_ref, parts_ref):
+    logits_ref[...] = logits + product(late_ref, weight_ref, 2, 0, 0)
+
+
+def far_kernel(shift, relayed_ref, late_ref, weight_ref, logits_ref, drafts_ref, before_ref, parts_ref):
     dp = before_ref.shape[0]
     copies = parts_ref.shape[0] // dp
     source = lax.rem(lax.axis_index("dp") + dp - shift, dp)
-    logits = logits_ref[...] + product(relayed_ref, weight_ref, 0, 1, 1) + product(second_ref, weight_ref, 1, 0, 1)
+    logits = logits_ref[...] + product(relayed_ref, weight_ref, 0, 1, 1) + product(late_ref, weight_ref, 2, 0, 1)
     totals, picks = contribution(logits, drafts_ref[...], source)
     for receiver in range(dp):
         part = before_ref[receiver] + parts_for(receiver, source, totals, picks)
@@ -165,74 +167,89 @@
     rows, depth = hidden.shape
     width = head_weight.shape[1]
     seqs, own_seqs = drafts.shape[0], rows // POSITIONS
-    second = depth // 2 - 2 * RELAYED
+    late_size = depth // 2 - 2 * RELAYED - EARLY
     lines = payload_lines(seqs, own_seqs)
     params = pltpu.CompilerParams(vmem_limit_bytes=GRANT)
     cost = pl.CostEstimate(
         flops=2 * rows * depth * width, bytes_accessed=2 * depth * (rows + width), transcendentals=2 * rows * width
     )
-    half_cost = pl.CostEstimate(
-        flops=rows * depth * width, bytes_accessed=depth * (rows + width), transcendentals=0
+    third_cost = pl.CostEstimate(
+        flops=rows * depth * width // 2, bytes_accessed=depth * (rows + width) // 2, transcendentals=0
     )
     swap = [(i, i ^ 1) for i in range(vocab)]
     relay = [(i, i ^ 2) for i in range(vocab)]
-    pieces = pl.pallas_call(
+    first_piece, early_piece, late_piece = pl.pallas_call(
         pieces_kernel,
-        out_shape=[jax.ShapeDtypeStruct((rows, size), hidden.dtype) for size in (RELAYED, second)],
+        out_shape=[jax.ShapeDtypeStruct((rows, size), hidden.dtype) for size in (RELAYED, EARLY, late_size)],
         in_specs=[VMEM],
-        out_specs=[VMEM] * 2,
+        out_specs=[VMEM] * 3,
         compiler_params=params,
         name="pieces",
     )(hidden)
-    others = []
+    logits_shape = jax.ShapeDtypeStruct((rows, width), jnp.float32)
     for k in range(1, dp):
         shift = [(i, (i + k) % dp) for i in range(dp)]
-        first = lax.ppermute(pieces[0], "dp", shift)
-        both = lax.ppermute(pieces[1], "dp", shift)
+        first = lax.ppermute(first_piece, "dp", shift)
+        early = lax.ppermute(early_piece, "dp", shift)
+        late = lax.ppermute(late_piece, "dp", shift)
         relayed = lax.ppermute(first, "vocab", relay)
-        others.append((first, both, relayed, lax.ppermute(first, "vocab", swap)))
-    parts, held, tokens = pl.pallas_call(
-        own_kernel,
-        out_shape=(
-            jax.ShapeDtypeStruct((dp, lines, LANES), jnp.float32),
-            pltpu.VMEM(head_weight.shape, head_weight.dtype),
-            pltpu.VMEM((DRAFTS, seqs), drafts.dtype),
-        ),
-        in_specs=[VMEM, pl.BlockSpec(memory_space=pl.ANY), pl.BlockSpec(memory_space=pl.ANY)],
-        out_specs=(VMEM,) * 3,
-        scratch_shapes=[pltpu.SemaphoreType.DMA((CHUNKS,)), pltpu.SemaphoreType.DMA],
-        cost_estimate=cost,
-        compiler_params=params,
-        name="own_rows",
-    )(
-        hidden,
-        pltpu.with_memory_space_constraint(head_weight, pltpu.HBM),
-        pltpu.with_memory_space_constraint(drafts.T, pltpu.HBM),
-    )
-    for k in range(1, dp):
-        first, both, relayed, first_swapped = others[k - 1]
-        both, relayed, first_swapped = lax.optimization_barrier((both, relayed, first_swapped))
-        relayed_swapped = lax.ppermute(relayed, "vocab", swap)
-        both_swapped = lax.ppermute(both, "vocab", swap)
-        count = dp * vocab if k == dp - 1 else dp
+        first_swapped = lax.ppermute(first, "vocab", swap)
+        if k == 1:
+            tokens = pl.pallas_call(
+                tokens_kernel,
+                out_shape=pltpu.VMEM((DRAFTS, seqs), drafts.dtype),
+                in_specs=[pl.BlockSpec(memory_space=pl.ANY)],
+                out_specs=VMEM,
+                scratch_shapes=[pltpu.SemaphoreType.DMA],
+                cost_estimate=pl.CostEstimate(flops=WEIGHT_HINT, bytes_accessed=0, transcendentals=0),
+                compiler_params=params,
+                name="tokens",
+            )(pltpu.with_memory_space_constraint(drafts.T, pltpu.HBM))
+            parts = pl.pallas_call(
+                own_kernel,
+                out_shape=jax.ShapeDtypeStruct((dp, lines, LANES), jnp.float32),
+                in_specs=[VMEM] * 3,
+                out_specs=VMEM,
+                cost_estimate=cost,
+                compiler_params=params,
+                name="own_rows",
+            )(hidden, head_weight, tokens)
+        early, first_swapped = lax.optimization_barrier((early, first_swapped))
+        early_swapped = lax.ppermute(early, "vocab", swap)
         logits = pl.pallas_call(
             near_kernel,
-            out_shape=jax.ShapeDtypeStruct((rows, width), jnp.float32),
+            out_shape=logits_shape,
+            in_specs=[VMEM] * 4,
+            out_specs=VMEM,
+            cost_estimate=third_cost,
+            compiler_params=params,
+            name="near",
+        )(first, first_swapped, early, head_weight)
+        late, relayed, logits = lax.optimization_barrier((late, relayed, logits))
+        relayed_swapped = lax.ppermute(relayed, "vocab", swap)
+        late_swapped = lax.ppermute(late, "vocab", swap)
+        logits = pl.pallas_call(
+            middle_kernel,
+            out_shape=logits_shape,
             in_specs=[VMEM] * 5,
             out_specs=VMEM,
-            cost_estimate=half_cost,
+            cost_estimate=third_cost,
             compiler_params=params,
-            name="near",
-        )(first, first_swapped, relayed, both, held)
+            name="middle",
+        )(early_swapped, relayed, late, head_weight, logits)
+        count = dp * vocab if k == dp - 1 else dp
         parts = pl.pallas_call(
             functools.partial(far_kernel, k),
             out_shape=jax.ShapeDtypeStruct((count, lines, LANES), jnp.float32),
             in_specs=[VMEM] * 6,
             out_specs=VMEM,
-            cost_estimate=half_cost,
+            cost_estimate=third_cost,
             compiler_params=params,
             name="far",
-        )(relayed_swapped, both_swapped, held, logits, tokens, parts)
+        )(relayed_swapped, late_swapped, head_weight, logits, tokens, parts)
+        if k < dp - 1:
+            pieces = first_piece, early_piece, late_piece
+            (first_piece, early_piece, late_piece), parts = lax.optimization_barrier((pieces, parts))
     parts = lax.all_to_all(parts, ("dp", "vocab"), 0, 0)
     log_norm, logprob, expected, loss = pl.pallas_call(
         functools.partial(tail_kernel, seqs),

time: 35 us -> 33.9 us (0.969)
  waiting for transfers between devices: 9.65 us -> 4.36 us
  local copies, waits for them, and re-layouts: 1.12 us -> 4.27 us
  starting transfers between devices: 5.39 us -> 7.66 us
  Pallas kernels: 4.81 us -> 4.09 us
  blocking collectives: 13.2 us -> 12.6 us
    unnamed x4 -> x12, local copies, waits for them, and re-layouts: 1.12 us -> 4.27 us
    ppermute x4 -> x6, waiting for transfers between devices: 7.2 us -> 4.35 us  [the longest x1 4.34 us: local(): first = lax.ppermute(first_piece, 'dp', shift)]
    ppermute x4 -> x6, starting transfers between devices: 3.12 us -> 5.64 us  [the longest x1 3.03 us: local(): early = lax.ppermute(early_piece, 'dp', shift)]
    ppermute x1, waiting for transfers between devices: 2.45 us -> 0.01 us  [local(): relayed = lax.ppermute(first, 'vocab', relay)]
    all_to_all x1, blocking collectives: 13.2 us -> 12.6 us  [local(): parts = lax.all_to_all(parts, ('dp', 'vocab'), 0, 0)]
    pallas_call x2 -> x4, Pallas kernels: 3.43 us -> 2.89 us  [the longest x1 1.06 us: local(): pl.pallas_call(own_kernel, out_shape=jax.ShapeDtypeStruct((dp, lines, LAN...]
  transfers between devices with their start and end apart: 6 -> 8, of which waited for: 2 -> 1; matrix products, arithmetic and copies ran while one was open for 0% -> 0% of each run, Pallas kernels for 10% -> 9%
where the time goes in v4:
time: 33.9 us; the launch traced here: 33.7 us
  blocking collectives  12.6 us (37%)
  starting transfers between devices  7.66 us (23%)
  waiting for transfers between devices  4.36 us (13%)
  local copies, waits for them, and re-layouts  4.27 us (13%)
  Pallas kernels  4.09 us (12%)
  between operations  0.72 us (2%)
    all_to_all x1, blocking collectives, local(): parts = lax.all_to_all(parts, ('dp', 'vocab'), 0, 0)  12.6 us
    ppermute x1, waiting for transfers between devices, local(): first = lax.ppermute(first_piece, 'dp', shift)  4.34 us
    unnamed x12, local copies, waits for them, and re-layouts  4.27 us
    ppermute x1, starting transfers between devices, local(): early = lax.ppermute(early_piece, 'dp', shift)  3.03 us
    ppermute x1, starting transfers between devices, local(): late = lax.ppermute(late_piece, 'dp', shift)  1.95 us
    ppermute x1, starting transfers between devices, local(): relayed = lax.ppermute(first, 'vocab', relay)  1.8 us
    pallas_call x1, Pallas kernels, local(): pl.pallas_call(own_kernel, out_shape=jax.ShapeDtypeStruct((dp, lines, LAN...  1.06 us
    pallas_call x1, Pallas kernels, local(): pl.pallas_call(tokens_kernel, out_shape=pltpu.VMEM((DRAFTS, seqs), drafts...  0.91 us
  transfers between devices with their start and end apart: 8, of which 1 were waited for; matrix products, arithmetic and copies ran while one was open for 0% of the time, Pallas kernels for 9%

profile of v4, /device:TPU:0, one launch (start us, length us, event | category | flops | bytes accessed | tf_op | source)
XLA Modules:
  0.0 33.7 jit_solution(11326648110074282816)
XLA Ops:
  0.6 0.0 copy-start.1
  0.6 1.1 %copy-done.1 = bf16[80,4608]{1,0:T(8,128)(2,1)S(1)} copy-done((bf16[80,4608]{1,0:T(8,128)(2,1)S(1)}, bf16[80,4608]{1,0:T(8,128)(2,1)}, u32[]{:S(2)}) %copy-start.1) | copy-done | bytes 737304
  1.8 3.0 %collective-permute-start.3 = (bf16[80,1024]{1,0:T(8,128)(2,1)S(1)}, bf16[80,1024]{1,0:T(8,128)(2,1)S(1)}, u32[]{:S(2)}, u32[]{:S(2)}) collective-permute-start(bf16[80,1024]{1,0:T(8,128)(2,1)S(1)} %get-tuple-element.18), channel_id=1, source_target_pairs={{0,16},{16,0},{1,17},{17,1},{2,18},{18,2},{3,19},{19,3},{4,20},{20... | collective-permute-start | bytes 491528 | tf_op jit(solution)/shard_map/ppermute | solution.py:193
  4.8 0.1 collective-permute-start.1
  4.9 1.9 %collective-permute-start = (bf16[80,512]{1,0:T(8,128)(2,1)S(1)}, bf16[80,512]{1,0:T(8,128)(2,1)S(1)}, u32[]{:S(2)}, u32[]{:S(2)}) collective-permute-start(bf16[80,512]{1,0:T(8,128)(2,1)S(1)} %get-tuple-element.16), channel_id=1, source_target_pairs={{0,16},{16,0},{1,17},{17,1},{2,18},{18,2},{3,19},{19,3},{4,20},{20... | collective-permute-start | bytes 245768 | tf_op jit(solution)/shard_map/ppermute | solution.py:194
  6.8 4.3 %collective-permute-done.1.first_ref = bf16[80,384]{1,0:T(8,128)(2,1)S(1)} collective-permute-done((bf16[80,384]{1,0:T(8,128)(2,1)S(1)}, bf16[80,384]{1,0:T(8,128)(2,1)S(1)}, u32[]{:S(2)}, u32[]{:S(2)}) %collective-permute-start.1) | collective-permute-done | bytes 61472 | tf_op jit(solution)/shard_map/ppermute | solution.py:192
  11.2 0.0 collective-permute-start.4
  11.2 1.8 %collective-permute-start.2 = (bf16[80,384]{1,0:T(8,128)(2,1)S(1)}, bf16[80,384]{1,0:T(8,128)(2,1)S(1)}, u32[]{:S(2)}, u32[]{:S(2)}) collective-permute-start(bf16[80,384]{1,0:T(8,128)(2,1)S(1)} %collective-permute-done.1.first_ref), channel_id=1, source_target_pairs={{0,2},{1,3},{2,0},{3,1},{4,6},{5,7},{6,4},{7,5},{8,10},{9,11},{10,... | collective-permute-start | bytes 184328 | tf_op jit(solution)/shard_map/ppermute | solution.py:195
  13.0 0.2 collective-permute-start.7
  13.2 2.3 %copy-done = bf16[4608,512]{1,0:T(8,128)(2,1)S(1)} copy-done((bf16[4608,512]{1,0:T(8,128)(2,1)S(1)}, bf16[4608,512]{1,0:T(8,128)(2,1)}, u32[]{:S(2)}) %copy-start) | copy-done | bytes 4718616
  15.5 0.4 %near.1.before_ref = f32[80,512]{1,0:T(8,128)S(1)} custom-call(bf16[80,384]{1,0:T(8,128)(2,1)S(1)} %collective-permute-done.1.first_ref, bf16[80,384]{1,0:T(8,128)(2,1)S(1)} %collective-permute-done.4.swapped_ref, bf16[80,1024]{1,0:T(8,128)(2,1)S(1)} %collective-permute-done.3.early_ref, bf16[4608,512]{1,0:T(8,128)(2,1)S(1)} %copy-done), custom_call_target="tpu_custom_call" | custom-call | flops 94371840 | bytes 1363968 | tf_op jit(solution)/shard_map/near/pallas_call | solution.py:219
  16.0 0.3 %collective-permute-start.6 = (bf16[80,512]{1,0:T(8,128)(2,1)S(1)}, bf16[80,512]{1,0:T(8,128)(2,1)S(1)}, u32[]{:S(2)}, u32[]{:S(2)}) collective-permute-start(bf16[80,512]{1,0:T(8,128)(2,1)S(1)} %collective-permute-done.late_ref), channel_id=1, source_target_pairs={{0,1},{1,0},{2,3},{3,2},{4,5},{5,4},{6,7},{7,6},{8,9},{9,8},{10,11... | collective-permute-start | bytes 245768 | tf_op jit(solution)/shard_map/ppermute | solution.py:230
  16.4 0.2 collective-permute-start.5
  16.6 0.9 %tokens.1.tokens_ref.drafts_ref = s32[4,32]{1,0:T(4,128)S(1)} custom-call(s32[4,32]{1,0:T(4,128)} %bitcast.10), custom_call_target="tpu_custom_call" | custom-call | flops 3000000000 | tf_op jit(solution)/shard_map/tokens/pallas_call | solution.py:198
  17.5 0.2 slice-done
  17.7 0.3 %slice-done.1 = s8[524288]{0:T(1024)(128)(4,1)S(1)} async-done(((s8[4718592]{0:T(1024)(128)(4,1)}), s8[524288]{0:T(1024)(128)(4,1)S(1)}, s32[]{:S(2)}) %slice-start.1) | async-done | bytes 524312
  18.1 0.2 copy-done.2
  18.3 1.1 %own_rows.1.before_ref = f32[2,2,128]{2,1,0:T(2,128)S(1)} custom-call(bf16[80,4608]{1,0:T(8,128)(2,1)S(1)} %copy-done.2, bf16[4608,512]{1,0:T(8,128)(2,1)S(1)} %bitcast.7, s32[4,32]{1,0:T(4,128)S(1)} %tokens.1.tokens_ref.drafts_ref), custom_call_target="tpu_custom_call" | custom-call | flops 377487360 | bytes 5455872 | tf_op jit(solution)/shard_map/own_rows/pallas_call | solution.py:208
  19.4 0.0 copy-start.3
  19.4 0.5 %middle.1.logits_ref = f32[80,512]{1,0:T(8,128)S(1)} custom-call(bf16[80,1024]{1,0:T(8,128)(2,1)S(1)} %collective-permute-done.7.swapped_ref, bf16[80,384]{1,0:T(8,128)(2,1)S(1)} %collective-permute-done.2.relayed_ref, bf16[80,512]{1,0:T(8,128)(2,1)S(1)} %collective-permute-done.late_ref, bf16[4608,512]{1,0:T(8,128)(2,1)S(1)} %bitcast.7, ...), custom_call_target="tpu_custom_call" | custom-call | flops 94371840 | bytes 1363968 | tf_op jit(solution)/shard_map/middle/pallas_call | solution.py:231
  19.9 0.0 collective-permute-done.5.relayed_ref
  19.9 0.5 %far.1 = f32[32,2,128]{2,1,0:T(2,128)S(1)} custom-call(bf16[80,384]{1,0:T(8,128)(2,1)S(1)} %collective-permute-done.5.relayed_ref, bf16[80,512]{1,0:T(8,128)(2,1)S(1)} %collective-permute-done.6.late_ref, bf16[4608,512]{1,0:T(8,128)(2,1)S(1)} %bitcast.7, f32[80,512]{1,0:T(8,128)S(1)} %middle.1.logits_ref, s32[4,32]{1,0:T(4,128)S(1)} %tokens.1.tokens_ref.drafts_ref, ...), custom_call_target="tpu_custom_call" | custom-call | flops 94371840 | bytes 1363968 | tf_op jit(solution)/shard_map/far/pallas_call | solution.py:241
  20.4 12.6 %all_to_all.5.parts_ref = f32[32,2,128]{2,1,0:T(2,128)S(1)} all-to-all(f32[32,2,128]{2,1,0:T(2,128)S(1)} %far.1), channel_id=1, replica_groups=mesh['dp'=2,'vocab'=16] {'dp','vocab'}, dimensions={0} | all-to-all | bytes 65536 | tf_op jit(solution)/shard_map/all_to_all | solution.py:253
  33.0 0.7 %tail.1 = (f32[5,16]{1,0:T(8,128)}, f32[4,16]{1,0:T(4,128)}, f32[1,16]{1,0:T(1,128)}, f32[1,1]{1,0:T(1,128)}) custom-call(f32[32,2,128]{2,1,0:T(2,128)S(1)} %all_to_all.5.parts_ref, s32[4,16]{1,0:T(4,128)S(1)} %bitcast.8), custom_call_target="tpu_custom_call" | custom-call | tf_op jit(solution)/shard_map/tail/pallas_call | solution.py:254
  (13 shorter events, 0.0 us)
Async XLA Ops:
  0.6 1.1 %copy-start.1 = (bf16[80,4608]{1,0:T(8,128)(2,1)S(1)}, bf16[80,4608]{1,0:T(8,128)(2,1)}, u32[]{:S(2)}) copy-start(bf16[80,4608]{1,0:T(8,128)(2,1)} %hidden_ref.3) | copy-start | bytes 2211844
  1.8 11.2 %collective-permute-start.3 = (bf16[80,1024]{1,0:T(8,128)(2,1)S(1)}, bf16[80,1024]{1,0:T(8,128)(2,1)S(1)}, u32[]{:S(2)}, u32[]{:S(2)}) collective-permute-start(bf16[80,1024]{1,0:T(8,128)(2,1)S(1)} %get-tuple-element.18), channel_id=1, source_target_pairs={{0,16},{16,0},{1,17},{17,1},{2,18},{18,2},{3,19},{19,3},{4,20},{20... | collective-permute-start | bytes 491528 | tf_op jit(solution)/shard_map/ppermute | solution.py:193
  4.8 6.4 %collective-permute-start.1 = (bf16[80,384]{1,0:T(8,128)(2,1)S(1)}, bf16[80,384]{1,0:T(8,128)(2,1)S(1)}, u32[]{:S(2)}, u32[]{:S(2)}) collective-permute-start(bf16[80,384]{1,0:T(8,128)(2,1)S(1)} %get-tuple-element.17), channel_id=1, source_target_pairs={{0,16},{16,0},{1,17},{17,1},{2,18},{18,2},{3,19},{19,3},{4,20},{20... | collective-permute-start | bytes 184328 | tf_op jit(solution)/shard_map/ppermute | solution.py:192
  4.9 11.1 %collective-permute-start = (bf16[80,512]{1,0:T(8,128)(2,1)S(1)}, bf16[80,512]{1,0:T(8,128)(2,1)S(1)}, u32[]{:S(2)}, u32[]{:S(2)}) collective-permute-start(bf16[80,512]{1,0:T(8,128)(2,1)S(1)} %get-tuple-element.16), channel_id=1, source_target_pairs={{0,16},{16,0},{1,17},{17,1},{2,18},{18,2},{3,19},{19,3},{4,20},{20... | collective-permute-start | bytes 245768 | tf_op jit(solution)/shard_map/ppermute | solution.py:194
  11.2 1.8 %collective-permute-start.4 = (bf16[80,384]{1,0:T(8,128)(2,1)S(1)}, bf16[80,384]{1,0:T(8,128)(2,1)S(1)}, u32[]{:S(2)}, u32[]{:S(2)}) collective-permute-start(bf16[80,384]{1,0:T(8,128)(2,1)S(1)} %collective-permute-done.1.first_ref), channel_id=1, source_target_pairs={{0,1},{1,0},{2,3},{3,2},{4,5},{5,4},{6,7},{7,6},{8,9},{9,8},{10,11... | collective-permute-start | bytes 184328 | tf_op jit(solution)/shard_map/ppermute | solution.py:196
  11.2 4.8 %collective-permute-start.2 = (bf16[80,384]{1,0:T(8,128)(2,1)S(1)}, bf16[80,384]{1,0:T(8,128)(2,1)S(1)}, u32[]{:S(2)}, u32[]{:S(2)}) collective-permute-start(bf16[80,384]{1,0:T(8,128)(2,1)S(1)} %collective-permute-done.1.first_ref), channel_id=1, source_target_pairs={{0,2},{1,3},{2,0},{3,1},{4,6},{5,7},{6,4},{7,5},{8,10},{9,11},{10,... | collective-permute-start | bytes 184328 | tf_op jit(solution)/shard_map/ppermute | solution.py:195
  13.0 6.4 %collective-permute-start.7 = (bf16[80,1024]{1,0:T(8,128)(2,1)S(1)}, bf16[80,1024]{1,0:T(8,128)(2,1)S(1)}, u32[]{:S(2)}, u32[]{:S(2)}) collective-permute-start(bf16[80,1024]{1,0:T(8,128)(2,1)S(1)} %collective-permute-done.3.early_ref), channel_id=1, source_target_pairs={{0,1},{1,0},{2,3},{3,2},{4,5},{5,4},{6,7},{7,6},{8,9},{9,8},{10,11... | collective-permute-start | bytes 491528 | tf_op jit(solution)/shard_map/ppermute | solution.py:218
  13.2 2.3 %copy-start = (bf16[4608,512]{1,0:T(8,128)(2,1)S(1)}, bf16[4608,512]{1,0:T(8,128)(2,1)}, u32[]{:S(2)}) copy-start(bf16[4608,512]{1,0:T(8,128)(2,1)} %weight_ref.7) | copy-start | bytes 14155780
  15.5 2.2 %slice-start = ((s8[4718592]{0:T(1024)(128)(4,1)}), s8[4194304]{0:T(1024)(128)(4,1)S(1)}, s32[]{:S(2)}) async-start(s8[4718592]{0:T(1024)(128)(4,1)} %bitcast.6), calls=%async_computation.1 | async-start | bytes 8388608
  16.0 3.9 %collective-permute-start.6 = (bf16[80,512]{1,0:T(8,128)(2,1)S(1)}, bf16[80,512]{1,0:T(8,128)(2,1)S(1)}, u32[]{:S(2)}, u32[]{:S(2)}) collective-permute-start(bf16[80,512]{1,0:T(8,128)(2,1)S(1)} %collective-permute-done.late_ref), channel_id=1, source_target_pairs={{0,1},{1,0},{2,3},{3,2},{4,5},{5,4},{6,7},{7,6},{8,9},{9,8},{10,11... | collective-permute-start | bytes 245768 | tf_op jit(solution)/shard_map/ppermute | solution.py:230
  16.4 3.5 %collective-permute-start.5 = (bf16[80,384]{1,0:T(8,128)(2,1)S(1)}, bf16[80,384]{1,0:T(8,128)(2,1)S(1)}, u32[]{:S(2)}, u32[]{:S(2)}) collective-permute-start(bf16[80,384]{1,0:T(8,128)(2,1)S(1)} %collective-permute-done.2.relayed_ref), channel_id=1, source_target_pairs={{0,1},{1,0},{2,3},{3,2},{4,5},{5,4},{6,7},{7,6},{8,9},{9,8},{10,11... | collective-permute-start | bytes 184328 | tf_op jit(solution)/shard_map/ppermute | solution.py:229
  16.6 1.5 %slice-start.1 = ((s8[4718592]{0:T(1024)(128)(4,1)}), s8[524288]{0:T(1024)(128)(4,1)S(1)}, s32[]{:S(2)}) async-start(s8[4718592]{0:T(1024)(128)(4,1)} %bitcast.6), calls=%async_computation.2 | async-start | bytes 1048576
  16.6 1.7 %copy-start.2 = (bf16[80,4608]{1,0:T(8,128)(2,1)S(1)}, bf16[80,4608]{1,0:T(8,128)(2,1)}, u32[]{:S(2)}) copy-start(bf16[80,4608]{1,0:T(8,128)(2,1)} %hidden_ref.3) | copy-start | bytes 2211844
  19.4 13.6 %copy-start.3 = (s32[16,4]{0,1:T(4,128)S(1)}, s32[16,4]{0,1:T(4,128)}, u32[]{:S(2)}) copy-start(s32[16,4]{0,1:T(4,128)} %param.7) | copy-start | bytes 772

commit v5 on v4

--- a/solution.py
+++ b/solution.py
@@ -13,9 +13,11 @@
 SOFT_CAP = 30.0
 Z_WEIGHT = 0.001
 LANES = 128
+SUBLANES = 8
 GRANT = 16 * 2**20
 RELAYED = 3 * LANES
 EARLY = 8 * LANES
+HIDDEN_HINT = 1_200_000_000
 WEIGHT_HINT = 3_000_000_000
 VMEM = pl.BlockSpec(memory_space=pltpu.VMEM)
 ANY = pl.BlockSpec(memory_space=pl.ANY)
@@ -75,8 +77,21 @@
     return pl.multiple_of(base + core * size, LANES)
 
 
+def first_kernel(hidden_ref, piece_ref, arrived):
+    rows, size = piece_ref.shape
+    columns = pl.ds(place(size, 0, 0, 0), size)
+    groups = [pl.ds(i, SUBLANES) for i in range(0, rows, SUBLANES)]
+    copies = [
+        pltpu.make_async_copy(hidden_ref.at[g, columns], piece_ref.at[g], arrived.at[i]) for i, g in enumerate(groups)
+    ]
+    for copy in copies:
+        copy.start()
+    for copy in copies:
+        copy.wait()
+
+
 def pieces_kernel(hidden_ref, *piece_refs):
-    for piece, ref in enumerate(piece_refs):
+    for piece, ref in enumerate(piece_refs, 1):
         size = ref.shape[1]
         ref[...] = hidden_ref[:, pl.ds(place(size, piece, 0, 0), size)]
 
@@ -178,11 +193,21 @@
     )
     swap = [(i, i ^ 1) for i in range(vocab)]
     relay = [(i, i ^ 2) for i in range(vocab)]
-    first_piece, early_piece, late_piece = pl.pallas_call(
+    first_piece = pl.pallas_call(
+        first_kernel,
+        out_shape=jax.ShapeDtypeStruct((rows, RELAYED), hidden.dtype),
+        in_specs=[pl.BlockSpec(memory_space=pl.ANY)],
+        out_specs=VMEM,
+        scratch_shapes=[pltpu.SemaphoreType.DMA((rows // SUBLANES,))],
+        cost_estimate=pl.CostEstimate(flops=HIDDEN_HINT, bytes_accessed=0, transcendentals=0),
+        compiler_params=params,
+        name="first_piece",
+    )(pltpu.with_memory_space_constraint(hidden, pltpu.HBM))
+    early_piece, late_piece = pl.pallas_call(
         pieces_kernel,
-        out_shape=[jax.ShapeDtypeStruct((rows, size), hidden.dtype) for size in (RELAYED, EARLY, late_size)],
+        out_shape=[jax.ShapeDtypeStruct((rows, size), hidden.dtype) for size in (EARLY, late_size)],
         in_specs=[VMEM],
-        out_specs=[VMEM] * 3,
+        out_specs=[VMEM] * 2,
         compiler_params=params,
         name="pieces",
     )(hidden)

time: 33.9 us -> 33.7 us (level)
  local copies, waits for them, and re-layouts: 4.27 us -> 1.63 us
  waiting for transfers between devices: 4.36 us -> 5.35 us
  Pallas kernels: 4.09 us -> 4.86 us
  blocking collectives: 12.6 us -> 13.1 us
    unnamed x12 -> x8, local copies, waits for them, and re-layouts: 4.27 us -> 1.63 us
    ppermute x1, waiting for transfers between devices: 0.01 us -> 1.98 us  [local(): relayed = lax.ppermute(first, 'vocab', relay)]
    ppermute x1, waiting for transfers between devices: 4.34 us -> 3.35 us  [local(): first = lax.ppermute(first_piece, 'dp', shift)]
    pallas_call x0 -> x1, Pallas kernels: none -> 0.91 us  [local(): pl.pallas_call(first_kernel, out_shape=jax.ShapeDtypeStruct((rows, RELAYE...]
    all_to_all x1, blocking collectives: 12.6 us -> 13.1 us  [local(): parts = lax.all_to_all(parts, ('dp', 'vocab'), 0, 0)]
    ppermute x1, starting transfers between devices: 0.35 us -> 0.01 us  [local(): late_swapped = lax.ppermute(late, 'vocab', swap)]
  transfers between devices with their start and end apart: 8 -> 8, of which waited for: 1 -> 2; matrix products, arithmetic and copies ran while one was open for 0% -> 0% of each run, Pallas kernels for 9% -> 11%
where the time goes in v5:
time: 33.7 us; the launch traced here: 33.4 us
  blocking collectives  13.1 us (39%)
  starting transfers between devices  7.66 us (23%)
  waiting for transfers between devices  5.35 us (16%)
  Pallas kernels  4.86 us (14%)
  local copies, waits for them, and re-layouts  1.63 us (5%)
  between operations  0.73 us (2%)
    all_to_all x1, blocking collectives, local(): parts = lax.all_to_all(parts, ('dp', 'vocab'), 0, 0)  13.1 us
    ppermute x1, waiting for transfers between devices, local(): first = lax.ppermute(first_piece, 'dp', shift)  3.35 us
    ppermute x1, starting transfers between devices, local(): early = lax.ppermute(early_piece, 'dp', shift)  3.03 us
    ppermute x1, waiting for transfers between devices, local(): relayed = lax.ppermute(first, 'vocab', relay)  1.98 us
    ppermute x1, starting transfers between devices, local(): relayed = lax.ppermute(first, 'vocab', relay)  1.8 us
    ppermute x1, starting transfers between devices, local(): late = lax.ppermute(late_piece, 'dp', shift)  1.76 us
    unnamed x8, local copies, waits for them, and re-layouts  1.63 us
    pallas_call x1, Pallas kernels, local(): pl.pallas_call(own_kernel, out_shape=jax.ShapeDtypeStruct((dp, lines, LAN...  1.07 us
  transfers between devices with their start and end apart: 8, of which 2 were waited for; matrix products, arithmetic and copies ran while one was open for 0% of the time, Pallas kernels for 11%

profile of v5, /device:TPU:0, one launch (start us, length us, event | category | flops | bytes accessed | tf_op | source)
XLA Modules:
  0.0 33.4 jit_solution(11949600074621474925)
XLA Ops:
  0.6 0.0 copy-start.1
  0.7 1.3 %copy-done.1 = bf16[80,4608]{1,0:T(8,128)(2,1)S(1)} copy-done((bf16[80,4608]{1,0:T(8,128)(2,1)S(1)}, bf16[80,4608]{1,0:T(8,128)(2,1)}, u32[]{:S(2)}) %copy-start.1) | copy-done | bytes 737304
  1.9 3.0 %collective-permute-start.3 = (bf16[80,1024]{1,0:T(8,128)(2,1)S(1)}, bf16[80,1024]{1,0:T(8,128)(2,1)S(1)}, u32[]{:S(2)}, u32[]{:S(2)}) collective-permute-start(bf16[80,1024]{1,0:T(8,128)(2,1)S(1)} %get-tuple-element.16), channel_id=1, source_target_pairs={{0,16},{16,0},{1,17},{17,1},{2,18},{18,2},{3,19},{19,3},{4,20},{20... | collective-permute-start | bytes 491528 | tf_op jit(solution)/shard_map/ppermute | solution.py:218
  5.0 0.9 %first_piece.1 = bf16[80,384]{1,0:T(8,128)(2,1)S(1)} custom-call(bf16[80,4608]{1,0:T(8,128)(2,1)} %hidden_ref.5), custom_call_target="tpu_custom_call" | custom-call | flops 1200000000 | tf_op jit(solution)/shard_map/first_piece/pallas_call | solution.py:196
  5.9 0.3 collective-permute-start.1
  6.2 1.8 %collective-permute-start = (bf16[80,512]{1,0:T(8,128)(2,1)S(1)}, bf16[80,512]{1,0:T(8,128)(2,1)S(1)}, u32[]{:S(2)}, u32[]{:S(2)}) collective-permute-start(bf16[80,512]{1,0:T(8,128)(2,1)S(1)} %get-tuple-element.15), channel_id=1, source_target_pairs={{0,16},{16,0},{1,17},{17,1},{2,18},{18,2},{3,19},{19,3},{4,20},{20... | collective-permute-start | bytes 245768 | tf_op jit(solution)/shard_map/ppermute | solution.py:219
  8.0 3.4 %collective-permute-done.1.first_ref = bf16[80,384]{1,0:T(8,128)(2,1)S(1)} collective-permute-done((bf16[80,384]{1,0:T(8,128)(2,1)S(1)}, bf16[80,384]{1,0:T(8,128)(2,1)S(1)}, u32[]{:S(2)}, u32[]{:S(2)}) %collective-permute-start.1) | collective-permute-done | bytes 61472 | tf_op jit(solution)/shard_map/ppermute | solution.py:217
  11.3 0.0 collective-permute-start.4
  11.3 1.8 %collective-permute-start.2 = (bf16[80,384]{1,0:T(8,128)(2,1)S(1)}, bf16[80,384]{1,0:T(8,128)(2,1)S(1)}, u32[]{:S(2)}, u32[]{:S(2)}) collective-permute-start(bf16[80,384]{1,0:T(8,128)(2,1)S(1)} %collective-permute-done.1.first_ref), channel_id=1, source_target_pairs={{0,2},{1,3},{2,0},{3,1},{4,6},{5,7},{6,4},{7,5},{8,10},{9,11},{10,... | collective-permute-start | bytes 184328 | tf_op jit(solution)/shard_map/ppermute | solution.py:220
  13.1 0.0 collective-permute-done.4.swapped_ref
  13.1 0.0 collective-permute-done.3.early_ref
  13.1 0.2 collective-permute-start.7
  13.4 0.4 %near.1.before_ref = f32[80,512]{1,0:T(8,128)S(1)} custom-call(bf16[80,384]{1,0:T(8,128)(2,1)S(1)} %collective-permute-done.1.first_ref, bf16[80,384]{1,0:T(8,128)(2,1)S(1)} %collective-permute-done.4.swapped_ref, bf16[80,1024]{1,0:T(8,128)(2,1)S(1)} %collective-permute-done.3.early_ref, bf16[4608,512]{1,0:T(8,128)(2,1)S(1)} %copy-done), custom_call_target="tpu_custom_call" | custom-call | flops 94371840 | bytes 1363968 | tf_op jit(solution)/shard_map/near/pallas_call | solution.py:244
  13.8 0.0 collective-permute-done.late_ref
  13.8 2.0 %collective-permute-done.2.relayed_ref = bf16[80,384]{1,0:T(8,128)(2,1)S(1)} collective-permute-done((bf16[80,384]{1,0:T(8,128)(2,1)S(1)}, bf16[80,384]{1,0:T(8,128)(2,1)S(1)}, u32[]{:S(2)}, u32[]{:S(2)}) %collective-permute-start.2) | collective-permute-done | bytes 61472 | tf_op jit(solution)/shard_map/ppermute | solution.py:220
  15.8 0.5 %collective-permute-start.5 = (bf16[80,384]{1,0:T(8,128)(2,1)S(1)}, bf16[80,384]{1,0:T(8,128)(2,1)S(1)}, u32[]{:S(2)}, u32[]{:S(2)}) collective-permute-start(bf16[80,384]{1,0:T(8,128)(2,1)S(1)} %collective-permute-done.2.relayed_ref), channel_id=1, source_target_pairs={{0,1},{1,0},{2,3},{3,2},{4,5},{5,4},{6,7},{7,6},{8,9},{9,8},{10,11... | collective-permute-start | bytes 184328 | tf_op jit(solution)/shard_map/ppermute | solution.py:254
  16.3 0.8 %tokens.1.tokens_ref.drafts_ref = s32[4,32]{1,0:T(4,128)S(1)} custom-call(s32[4,32]{1,0:T(4,128)} %bitcast.8), custom_call_target="tpu_custom_call" | custom-call | flops 3000000000 | tf_op jit(solution)/shard_map/tokens/pallas_call | solution.py:223
  17.1 0.4 %copy-done.2 = bf16[80,4608]{1,0:T(8,128)(2,1)S(1)} copy-done((bf16[80,4608]{1,0:T(8,128)(2,1)S(1)}, bf16[80,4608]{1,0:T(8,128)(2,1)}, u32[]{:S(2)}) %copy-start.2) | copy-done | bytes 737304
  17.4 1.1 %own_rows.1.before_ref = f32[2,2,128]{2,1,0:T(2,128)S(1)} custom-call(bf16[80,4608]{1,0:T(8,128)(2,1)S(1)} %copy-done.2, bf16[4608,512]{1,0:T(8,128)(2,1)S(1)} %copy-done, s32[4,32]{1,0:T(4,128)S(1)} %tokens.1.tokens_ref.drafts_ref), custom_call_target="tpu_custom_call" | custom-call | flops 377487360 | bytes 5455872 | tf_op jit(solution)/shard_map/own_rows/pallas_call | solution.py:233
  18.5 0.0 copy-start.3
  18.5 0.5 %middle.1.logits_ref = f32[80,512]{1,0:T(8,128)S(1)} custom-call(bf16[80,1024]{1,0:T(8,128)(2,1)S(1)} %collective-permute-done.7.swapped_ref, bf16[80,384]{1,0:T(8,128)(2,1)S(1)} %collective-permute-done.2.relayed_ref, bf16[80,512]{1,0:T(8,128)(2,1)S(1)} %collective-permute-done.late_ref, bf16[4608,512]{1,0:T(8,128)(2,1)S(1)} %copy-done, ...), custom_call_target="tpu_custom_call" | custom-call | flops 94371840 | bytes 1363968 | tf_op jit(solution)/shard_map/middle/pallas_call | solution.py:256
  19.0 0.5 %far.1 = f32[32,2,128]{2,1,0:T(2,128)S(1)} custom-call(bf16[80,384]{1,0:T(8,128)(2,1)S(1)} %collective-permute-done.5.relayed_ref, bf16[80,512]{1,0:T(8,128)(2,1)S(1)} %collective-permute-done.6.late_ref, bf16[4608,512]{1,0:T(8,128)(2,1)S(1)} %copy-done, f32[80,512]{1,0:T(8,128)S(1)} %middle.1.logits_ref, s32[4,32]{1,0:T(4,128)S(1)} %tokens.1.tokens_ref.drafts_ref, ...), custom_call_target="tpu_custom_call" | custom-call | flops 94371840 | bytes 1363968 | tf_op jit(solution)/shard_map/far/pallas_call | solution.py:266
  19.5 13.1 %all_to_all.5.parts_ref = f32[32,2,128]{2,1,0:T(2,128)S(1)} all-to-all(f32[32,2,128]{2,1,0:T(2,128)S(1)} %far.1), channel_id=1, replica_groups=mesh['dp'=2,'vocab'=16] {'dp','vocab'}, dimensions={0} | all-to-all | bytes 65536 | tf_op jit(solution)/shard_map/all_to_all | solution.py:278
  32.7 0.7 %tail.1 = (f32[5,16]{1,0:T(8,128)}, f32[4,16]{1,0:T(4,128)}, f32[1,16]{1,0:T(1,128)}, f32[1,1]{1,0:T(1,128)}) custom-call(f32[32,2,128]{2,1,0:T(2,128)S(1)} %all_to_all.5.parts_ref, s32[4,16]{1,0:T(4,128)S(1)} %bitcast.6), custom_call_target="tpu_custom_call" | custom-call | tf_op jit(solution)/shard_map/tail/pallas_call | solution.py:279
  (9 shorter events, 0.0 us)
Async XLA Ops:
  0.6 12.7 %copy-start = (bf16[4608,512]{1,0:T(8,128)(2,1)S(1)}, bf16[4608,512]{1,0:T(8,128)(2,1)}, u32[]{:S(2)}) copy-start(bf16[4608,512]{1,0:T(8,128)(2,1)} %weight_ref.7) | copy-start | bytes 14155780
  0.6 1.3 %copy-start.1 = (bf16[80,4608]{1,0:T(8,128)(2,1)S(1)}, bf16[80,4608]{1,0:T(8,128)(2,1)}, u32[]{:S(2)}) copy-start(bf16[80,4608]{1,0:T(8,128)(2,1)} %hidden_ref.5) | copy-start | bytes 2211844
  1.9 11.2 %collective-permute-start.3 = (bf16[80,1024]{1,0:T(8,128)(2,1)S(1)}, bf16[80,1024]{1,0:T(8,128)(2,1)S(1)}, u32[]{:S(2)}, u32[]{:S(2)}) collective-permute-start(bf16[80,1024]{1,0:T(8,128)(2,1)S(1)} %get-tuple-element.16), channel_id=1, source_target_pairs={{0,16},{16,0},{1,17},{17,1},{2,18},{18,2},{3,19},{19,3},{4,20},{20... | collective-permute-start | bytes 491528 | tf_op jit(solution)/shard_map/ppermute | solution.py:218
  5.9 5.4 %collective-permute-start.1 = (bf16[80,384]{1,0:T(8,128)(2,1)S(1)}, bf16[80,384]{1,0:T(8,128)(2,1)S(1)}, u32[]{:S(2)}, u32[]{:S(2)}) collective-permute-start(bf16[80,384]{1,0:T(8,128)(2,1)S(1)} %first_piece.1), channel_id=1, source_target_pairs={{0,16},{16,0},{1,17},{17,1},{2,18},{18,2},{3,19},{19,3},{4,20},{20... | collective-permute-start | bytes 184328 | tf_op jit(solution)/shard_map/ppermute | solution.py:217
  6.2 7.6 %collective-permute-start = (bf16[80,512]{1,0:T(8,128)(2,1)S(1)}, bf16[80,512]{1,0:T(8,128)(2,1)S(1)}, u32[]{:S(2)}, u32[]{:S(2)}) collective-permute-start(bf16[80,512]{1,0:T(8,128)(2,1)S(1)} %get-tuple-element.15), channel_id=1, source_target_pairs={{0,16},{16,0},{1,17},{17,1},{2,18},{18,2},{3,19},{19,3},{4,20},{20... | collective-permute-start | bytes 245768 | tf_op jit(solution)/shard_map/ppermute | solution.py:219
  11.3 1.8 %collective-permute-start.4 = (bf16[80,384]{1,0:T(8,128)(2,1)S(1)}, bf16[80,384]{1,0:T(8,128)(2,1)S(1)}, u32[]{:S(2)}, u32[]{:S(2)}) collective-permute-start(bf16[80,384]{1,0:T(8,128)(2,1)S(1)} %collective-permute-done.1.first_ref), channel_id=1, source_target_pairs={{0,1},{1,0},{2,3},{3,2},{4,5},{5,4},{6,7},{7,6},{8,9},{9,8},{10,11... | collective-permute-start | bytes 184328 | tf_op jit(solution)/shard_map/ppermute | solution.py:221
  11.3 4.5 %collective-permute-start.2 = (bf16[80,384]{1,0:T(8,128)(2,1)S(1)}, bf16[80,384]{1,0:T(8,128)(2,1)S(1)}, u32[]{:S(2)}, u32[]{:S(2)}) collective-permute-start(bf16[80,384]{1,0:T(8,128)(2,1)S(1)} %collective-permute-done.1.first_ref), channel_id=1, source_target_pairs={{0,2},{1,3},{2,0},{3,1},{4,6},{5,7},{6,4},{7,5},{8,10},{9,11},{10,... | collective-permute-start | bytes 184328 | tf_op jit(solution)/shard_map/ppermute | solution.py:220
  13.1 5.4 %collective-permute-start.7 = (bf16[80,1024]{1,0:T(8,128)(2,1)S(1)}, bf16[80,1024]{1,0:T(8,128)(2,1)S(1)}, u32[]{:S(2)}, u32[]{:S(2)}) collective-permute-start(bf16[80,1024]{1,0:T(8,128)(2,1)S(1)} %collective-permute-done.3.early_ref), channel_id=1, source_target_pairs={{0,1},{1,0},{2,3},{3,2},{4,5},{5,4},{6,7},{7,6},{8,9},{9,8},{10,11... | collective-permute-start | bytes 491528 | tf_op jit(solution)/shard_map/ppermute | solution.py:243
  15.8 3.2 %collective-permute-start.6 = (bf16[80,512]{1,0:T(8,128)(2,1)S(1)}, bf16[80,512]{1,0:T(8,128)(2,1)S(1)}, u32[]{:S(2)}, u32[]{:S(2)}) collective-permute-start(bf16[80,512]{1,0:T(8,128)(2,1)S(1)} %collective-permute-done.late_ref), channel_id=1, source_target_pairs={{0,1},{1,0},{2,3},{3,2},{4,5},{5,4},{6,7},{7,6},{8,9},{9,8},{10,11... | collective-permute-start | bytes 245768 | tf_op jit(solution)/shard_map/ppermute | solution.py:255
  15.8 3.2 %collective-permute-start.5 = (bf16[80,384]{1,0:T(8,128)(2,1)S(1)}, bf16[80,384]{1,0:T(8,128)(2,1)S(1)}, u32[]{:S(2)}, u32[]{:S(2)}) collective-permute-start(bf16[80,384]{1,0:T(8,128)(2,1)S(1)} %collective-permute-done.2.relayed_ref), channel_id=1, source_target_pairs={{0,1},{1,0},{2,3},{3,2},{4,5},{5,4},{6,7},{7,6},{8,9},{9,8},{10,11... | collective-permute-start | bytes 184328 | tf_op jit(solution)/shard_map/ppermute | solution.py:254
  16.3 1.1 %copy-start.2 = (bf16[80,4608]{1,0:T(8,128)(2,1)S(1)}, bf16[80,4608]{1,0:T(8,128)(2,1)}, u32[]{:S(2)}) copy-start(bf16[80,4608]{1,0:T(8,128)(2,1)} %hidden_ref.5) | copy-start | bytes 2211844
  18.5 14.1 %copy-start.3 = (s32[16,4]{0,1:T(4,128)S(1)}, s32[16,4]{0,1:T(4,128)}, u32[]{:S(2)}) copy-start(s32[16,4]{0,1:T(4,128)} %param.7) | copy-start | bytes 772

commit v6 on v5

--- a/solution.py
+++ b/solution.py
@@ -15,8 +15,8 @@
 LANES = 128
 SUBLANES = 8
 GRANT = 16 * 2**20
-RELAYED = 3 * LANES
-EARLY = 8 * LANES
+RELAYED = 6 * LANES
+EARLY = 16 * LANES
 HIDDEN_HINT = 1_200_000_000
 WEIGHT_HINT = 3_000_000_000
 VMEM = pl.BlockSpec(memory_space=pltpu.VMEM)
@@ -50,18 +50,21 @@
     return -(-(POSITIONS * seqs + DRAFTS * own_seqs) // LANES)
 
 
-def contribution(logits, drafts, source):
-    rows, width = logits.shape
-    seqs, own_seqs = drafts.shape[1], rows // POSITIONS
-    shard = lax.axis_index("dp") * lax.axis_size("vocab") + lax.axis_index("vocab")
-    ids = row_ids(drafts, rows, source * own_seqs) - shard * width
-    capped = SOFT_CAP * jnp.tanh(logits * (1.0 / SOFT_CAP))
-    totals = jnp.sum(jnp.exp(capped), axis=1, keepdims=True)
+def contribution(blocks, drafts, own_seqs, first_seq, local_seq):
+    rows, width = blocks[0][0].shape
+    seqs = drafts.shape[1]
+    ids = row_ids(drafts, rows, first_seq)
     columns = lax.broadcasted_iota(jnp.int32, (rows, width), 1)
-    picks = jnp.sum(jnp.where(columns == ids, capped, 0.0), axis=1, keepdims=True)
+    totals = picks = 0.0
+    for logits, shard in blocks:
+        capped = SOFT_CAP * jnp.tanh(logits * (1.0 / SOFT_CAP))
+        totals += jnp.exp(capped)
+        picks += jnp.where(columns == ids - shard * width, capped, 0.0)
+    totals = jnp.sum(totals, axis=1, keepdims=True)
+    picks = jnp.sum(picks, axis=1, keepdims=True)
     lines = payload_lines(seqs, own_seqs)
-    totals = spread(totals, [p * seqs + source * own_seqs for p in range(POSITIONS)], lines)
-    picks = spread(picks, [POSITIONS * seqs + p * own_seqs for p in range(DRAFTS)], lines)
+    totals = spread(totals, [p * seqs + first_seq for p in range(POSITIONS)], lines)
+    picks = spread(picks, [POSITIONS * seqs + p * own_seqs + local_seq for p in range(DRAFTS)], lines)
     return totals, picks
 
 
@@ -69,37 +72,36 @@
     return totals + jnp.where(source == receiver, picks, 0.0)
 
 
-def place(size, piece, other_row, other_core):
-    me = lax.axis_index("vocab")
-    core = lax.rem(me + other_core, 2)
-    row = lax.rem(me // 2 + other_row, 2)
-    base = (2 * row * RELAYED, 4 * RELAYED, 4 * RELAYED + 2 * EARLY)[piece]
-    return pl.multiple_of(base + core * size, LANES)
+def place(piece, other_row):
+    if piece:
+        return 2 * RELAYED + (piece - 1) * EARLY
+    row = lax.rem(lax.axis_index("vocab") // 2 + other_row, 2)
+    return pl.multiple_of(row * RELAYED, LANES)
+
+
+def half_start(rows):
+    return pl.multiple_of(lax.rem(lax.axis_index("vocab"), 2) * rows, SUBLANES)
 
 
 def first_kernel(hidden_ref, piece_ref, arrived):
     rows, size = piece_ref.shape
-    columns = pl.ds(place(size, 0, 0, 0), size)
-    groups = [pl.ds(i, SUBLANES) for i in range(0, rows, SUBLANES)]
-    copies = [
-        pltpu.make_async_copy(hidden_ref.at[g, columns], piece_ref.at[g], arrived.at[i]) for i, g in enumerate(groups)
-    ]
-    for copy in copies:
-        copy.start()
-    for copy in copies:
-        copy.wait()
+    source = hidden_ref.at[pl.ds(half_start(rows), rows), pl.ds(place(0, 0), size)]
+    copy = pltpu.make_async_copy(source, piece_ref, arrived)
+    copy.start()
+    copy.wait()
 
 
 def pieces_kernel(hidden_ref, *piece_refs):
     for piece, ref in enumerate(piece_refs, 1):
-        size = ref.shape[1]
-        ref[...] = hidden_ref[:, pl.ds(place(size, piece, 0, 0), size)]
-
-
-def product(rows_ref, weight_ref, piece, other_row, other_core):
-    size = rows_ref.shape[1]
-    block = weight_ref[pl.ds(place(size, piece, other_row, other_core), size), :]
-    return jnp.dot(rows_ref[...], block, preferred_element_type=jnp.float32)
+        rows, size = ref.shape
+        ref[...] = hidden_ref[pl.ds(half_start(rows), rows), pl.ds(place(piece, 0), size)]
+
+
+def product(rows_ref, weight_refs, piece, other_row):
+    block = pl.ds(place(piece, other_row), rows_ref.shape[1])
+    return jnp.concatenate(
+        [jnp.dot(rows_ref[...], w[block, :], preferred_element_type=jnp.float32) for w in weight_refs], axis=0
+    )
 
 
 def tokens_kernel(drafts_ref, tokens_ref, arrived):
@@ -111,28 +113,32 @@
 def own_kernel(hidden_ref, weight_ref, tokens_ref, parts_ref):
     logits = jnp.dot(hidden_ref[...], weight_ref[...], preferred_element_type=jnp.float32)
     me = lax.axis_index("dp")
-    totals, picks = contribution(logits, tokens_ref[...], me)
+    own_seqs = hidden_ref.shape[0] // POSITIONS
+    shard = me * lax.axis_size("vocab") + lax.axis_index("vocab")
+    totals, picks = contribution([(logits, shard)], tokens_ref[...], own_seqs, me * own_seqs, 0)
     for receiver in range(parts_ref.shape[0]):
         parts_ref[receiver] = parts_for(receiver, me, totals, picks)
 
 
-def near_kernel(first_ref, swapped_ref, early_ref, weight_ref, logits_ref):
-    logits = product(first_ref, weight_ref, 0, 0, 0) + product(swapped_ref, weight_ref, 0, 0, 1)
-    logits_ref[...] = logits + product(early_ref, weight_ref, 1, 0, 0)
-
-
-def middle_kernel(swapped_ref, relayed_ref, late_ref, weight_ref, before_ref, logits_ref):
-    logits = before_ref[...] + product(swapped_ref, weight_ref, 1, 0, 1)
-    logits += product(relayed_ref, weight_ref, 0, 1, 0)
-    logits_ref[...] = logits + product(late_ref, weight_ref, 2, 0, 0)
-
-
-def far_kernel(shift, relayed_ref, late_ref, weight_ref, logits_ref, drafts_ref, before_ref, parts_ref):
+def begin_kernel(rows_ref, weight_ref, other_ref, logits_ref):
+    logits_ref[...] = product(rows_ref, (weight_ref, other_ref), 0, 0)
+
+
+def add_kernel(piece, other_row, rows_ref, weight_ref, other_ref, before_ref, logits_ref):
+    logits_ref[...] = before_ref[...] + product(rows_ref, (weight_ref, other_ref), piece, other_row)
+
+
+def far_kernel(shift, late_ref, weight_ref, other_ref, logits_ref, tokens_ref, before_ref, parts_ref):
+    rows = late_ref.shape[0]
     dp = before_ref.shape[0]
     copies = parts_ref.shape[0] // dp
     source = lax.rem(lax.axis_index("dp") + dp - shift, dp)
-    logits = logits_ref[...] + product(relayed_ref, weight_ref, 0, 1, 1) + product(late_ref, weight_ref, 2, 0, 1)
-    totals, picks = contribution(logits, drafts_ref[...], source)
+    core = lax.rem(lax.axis_index("vocab"), 2)
+    shard = lax.axis_index("dp") * lax.axis_size("vocab") + lax.axis_index("vocab")
+    logits = logits_ref[...] + product(late_ref, (weight_ref, other_ref), 2, 0)
+    blocks = [(logits[:rows], shard), (logits[rows:], shard + 1 - 2 * core)]
+    seqs = rows // POSITIONS
+    totals, picks = contribution(blocks, tokens_ref[...], 2 * seqs, (2 * source + core) * seqs, core * seqs)
     for receiver in range(dp):
         part = before_ref[receiver] + parts_for(receiver, source, totals, picks)
         parts_ref[receiver * copies : (receiver + 1) * copies] = jnp.broadcast_to(part[None], (copies,) + part.shape)
@@ -182,7 +188,8 @@
     rows, depth = hidden.shape
     width = head_weight.shape[1]
     seqs, own_seqs = drafts.shape[0], rows // POSITIONS
-    late_size = depth // 2 - 2 * RELAYED - EARLY
+    late_size = depth - 2 * RELAYED - EARLY
+    half = rows // 2
     lines = payload_lines(seqs, own_seqs)
     params = pltpu.CompilerParams(vmem_limit_bytes=GRANT)
     cost = pl.CostEstimate(
@@ -195,17 +202,17 @@
     relay = [(i, i ^ 2) for i in range(vocab)]
     first_piece = pl.pallas_call(
         first_kernel,
-        out_shape=jax.ShapeDtypeStruct((rows, RELAYED), hidden.dtype),
+        out_shape=jax.ShapeDtypeStruct((half, RELAYED), hidden.dtype),
         in_specs=[pl.BlockSpec(memory_space=pl.ANY)],
         out_specs=VMEM,
-        scratch_shapes=[pltpu.SemaphoreType.DMA((rows // SUBLANES,))],
+        scratch_shapes=[pltpu.SemaphoreType.DMA],
         cost_estimate=pl.CostEstimate(flops=HIDDEN_HINT, bytes_accessed=0, transcendentals=0),
         compiler_params=params,
         name="first_piece",
     )(pltpu.with_memory_space_constraint(hidden, pltpu.HBM))
     early_piece, late_piece = pl.pallas_call(
         pieces_kernel,
-        out_shape=[jax.ShapeDtypeStruct((rows, size), hidden.dtype) for size in (EARLY, late_size)],
+        out_shape=[jax.ShapeDtypeStruct((half, size), hidden.dtype) for size in (EARLY, late_size)],
         in_specs=[VMEM],
         out_specs=[VMEM] * 2,
         compiler_params=params,
@@ -218,8 +225,8 @@
         early = lax.ppermute(early_piece, "dp", shift)
         late = lax.ppermute(late_piece, "dp", shift)
         relayed = lax.ppermute(first, "vocab", relay)
-        first_swapped = lax.ppermute(first, "vocab", swap)
         if k == 1:
+            other_weight = lax.ppermute(head_weight, "vocab", swap)
             tokens = pl.pallas_call(
                 tokens_kernel,
                 out_shape=pltpu.VMEM((DRAFTS, seqs), drafts.dtype),
@@ -239,29 +246,19 @@
                 compiler_params=params,
                 name="own_rows",
             )(hidden, head_weight, tokens)
-        early, first_swapped = lax.optimization_barrier((early, first_swapped))
-        early_swapped = lax.ppermute(early, "vocab", swap)
-        logits = pl.pallas_call(
-            near_kernel,
+        multiply = functools.partial(
+            pl.pallas_call,
             out_shape=logits_shape,
-            in_specs=[VMEM] * 4,
             out_specs=VMEM,
             cost_estimate=third_cost,
             compiler_params=params,
-            name="near",
-        )(first, first_swapped, early, head_weight)
-        late, relayed, logits = lax.optimization_barrier((late, relayed, logits))
-        relayed_swapped = lax.ppermute(relayed, "vocab", swap)
-        late_swapped = lax.ppermute(late, "vocab", swap)
-        logits = pl.pallas_call(
-            middle_kernel,
-            out_shape=logits_shape,
-            in_specs=[VMEM] * 5,
-            out_specs=VMEM,
-            cost_estimate=third_cost,
-            compiler_params=params,
-            name="middle",
-        )(early_swapped, relayed, late, head_weight, logits)
+        )
+        call = multiply(begin_kernel, in_specs=[VMEM] * 3, name="begin")
+        logits = call(first, head_weight, other_weight)
+        call = multiply(functools.partial(add_kernel, 1, 0), in_specs=[VMEM] * 4, name="near")
+        logits = call(early, head_weight, other_weight, logits)
+        call = multiply(functools.partial(add_kernel, 0, 1), in_specs=[VMEM] * 4, name="middle")
+        logits = call(relayed, head_weight, other_weight, logits)
         count = dp * vocab if k == dp - 1 else dp
         parts = pl.pallas_call(
             functools.partial(far_kernel, k),
@@ -271,7 +268,7 @@
             cost_estimate=third_cost,
             compiler_params=params,
             name="far",
-        )(relayed_swapped, late_swapped, head_weight, logits, tokens, parts)
+        )(late, head_weight, other_weight, logits, tokens, parts)
         if k < dp - 1:
             pieces = first_piece, early_piece, late_piece
             (first_piece, early_piece, late_piece), parts = lax.optimization_barrier((pieces, parts))

time: 33.7 us -> 28.5 us (0.85)
  waiting for transfers between devices: 5.35 us -> 1.68 us
  local copies, waits for them, and re-layouts: 1.63 us -> 0.31 us
  Pallas kernels: 4.86 us -> 5.58 us
  starting transfers between devices: 7.66 us -> 7.06 us
    ppermute x1, waiting for transfers between devices: 3.35 us -> 0.47 us  [local(): first = lax.ppermute(first_piece, 'dp', shift)]
    ppermute x1, starting transfers between devices: 0.33 us -> 2.64 us  [local(): first = lax.ppermute(first_piece, 'dp', shift)]
    ppermute x1, waiting for transfers between devices: 1.98 us -> 0.01 us  [local(): relayed = lax.ppermute(first, 'vocab', relay)]
    ppermute x1, starting transfers between devices: 1.76 us -> 0.13 us  [local(): late = lax.ppermute(late_piece, 'dp', shift)]
    unnamed x8, local copies, waits for them, and re-layouts: 1.63 us -> 0.31 us
    ppermute x1, waiting for transfers between devices: 0.01 us -> 1.2 us  [local(): early = lax.ppermute(early_piece, 'dp', shift)]
    ppermute x1, starting transfers between devices: 3.03 us -> 1.96 us  [local(): early = lax.ppermute(early_piece, 'dp', shift)]
    pallas_call x4 -> x5, Pallas kernels: 1.86 us -> 2.45 us  [the longest x1 0.84 us: local(): pl.pallas_call(first_kernel, out_shape=jax.ShapeDtypeStruct((half, RELAYE...]
  transfers between devices with their start and end apart: 8 -> 5, of which waited for: 2 -> 2; matrix products, arithmetic and copies ran while one was open for 0% -> 0% of each run, Pallas kernels for 11% -> 15%
where the time goes in v6:
time: 28.5 us; the launch traced here: 28.3 us
  blocking collectives  12.9 us (45%)
  starting transfers between devices  7.06 us (25%)
  Pallas kernels  5.58 us (20%)
  waiting for transfers between devices  1.68 us (6%)
  between operations  0.73 us (3%)
  local copies, waits for them, and re-layouts  0.31 us (1%)
    all_to_all x1, blocking collectives, local(): parts = lax.all_to_all(parts, ('dp', 'vocab'), 0, 0)  12.9 us
    ppermute x1, starting transfers between devices, local(): first = lax.ppermute(first_piece, 'dp', shift)  2.64 us
    ppermute x1, starting transfers between devices, local(): early = lax.ppermute(early_piece, 'dp', shift)  1.96 us
    ppermute x1, starting transfers between devices, local(): relayed = lax.ppermute(first, 'vocab', relay)  1.78 us
    ppermute x1, waiting for transfers between devices, local(): early = lax.ppermute(early_piece, 'dp', shift)  1.2 us
    pallas_call x1, Pallas kernels, local(): pl.pallas_call(own_kernel, out_shape=jax.ShapeDtypeStruct((dp, lines, LAN...  1.07 us
    pallas_call x1, Pallas kernels, local(): pl.pallas_call(first_kernel, out_shape=jax.ShapeDtypeStruct((half, RELAYE...  0.84 us
    pallas_call x1, Pallas kernels, local(): logits = call(early, head_weight, other_weight, logits)  0.82 us
  transfers between devices with their start and end apart: 5, of which 2 were waited for; matrix products, arithmetic and copies ran while one was open for 0% of the time, Pallas kernels for 15%

profile of v6, /device:TPU:0, one launch (start us, length us, event | category | flops | bytes accessed | tf_op | source)
XLA Modules:
  0.0 28.3 jit_solution(17629425951707391832)
XLA Ops:
  0.6 0.0 copy-start
  0.6 0.6 %collective-permute-start.1 = (bf16[4608,512]{1,0:T(8,128)(2,1)}, bf16[4608,512]{1,0:T(8,128)(2,1)S(1)}, u32[]{:S(2)}, u32[]{:S(2)}) collective-permute-start(bf16[4608,512]{1,0:T(8,128)(2,1)} %weight_ref.9), channel_id=1, source_target_pairs={{0,1},{1,0},{2,3},{3,2},{4,5},{5,4},{6,7},{7,6},{8,9},{9,8},{10,11... | collective-permute-start | bytes 14155784 | tf_op jit(solution)/shard_map/ppermute | solution.py:229
  1.2 0.8 %first_piece.1 = bf16[40,768]{1,0:T(8,128)(2,1)S(1)} custom-call(bf16[80,4608]{1,0:T(8,128)(2,1)} %hidden_ref.5), custom_call_target="tpu_custom_call" | custom-call | flops 1200000000 | tf_op jit(solution)/shard_map/first_piece/pallas_call | solution.py:203
  2.0 2.6 %collective-permute-start.2 = (bf16[40,768]{1,0:T(8,128)(2,1)S(1)}, bf16[40,768]{1,0:T(8,128)(2,1)S(1)}, u32[]{:S(2)}, u32[]{:S(2)}) collective-permute-start(bf16[40,768]{1,0:T(8,128)(2,1)S(1)} %first_piece.1), channel_id=1, source_target_pairs={{0,16},{16,0},{1,17},{17,1},{2,18},{18,2},{3,19},{19,3},{4,20},{20... | collective-permute-start | bytes 184328 | tf_op jit(solution)/shard_map/ppermute | solution.py:224
  4.7 0.0 copy-done
  4.7 0.1 collective-permute-start
  4.8 2.0 %collective-permute-start.4 = (bf16[40,2048]{1,0:T(8,128)(2,1)S(1)}, bf16[40,2048]{1,0:T(8,128)(2,1)S(1)}, u32[]{:S(2)}, u32[]{:S(2)}) collective-permute-start(bf16[40,2048]{1,0:T(8,128)(2,1)S(1)} %get-tuple-element.11), channel_id=1, source_target_pairs={{0,16},{16,0},{1,17},{17,1},{2,18},{18,2},{3,19},{19,3},{4,20},{20... | collective-permute-start | bytes 491528 | tf_op jit(solution)/shard_map/ppermute | solution.py:225
  6.8 0.5 %collective-permute-done.2.rows_ref = bf16[40,768]{1,0:T(8,128)(2,1)S(1)} collective-permute-done((bf16[40,768]{1,0:T(8,128)(2,1)S(1)}, bf16[40,768]{1,0:T(8,128)(2,1)S(1)}, u32[]{:S(2)}, u32[]{:S(2)}) %collective-permute-start.2) | collective-permute-done | bytes 61472 | tf_op jit(solution)/shard_map/ppermute | solution.py:224
  7.3 1.8 %collective-permute-start.3 = (bf16[40,768]{1,0:T(8,128)(2,1)S(1)}, bf16[40,768]{1,0:T(8,128)(2,1)S(1)}, u32[]{:S(2)}, u32[]{:S(2)}) collective-permute-start(bf16[40,768]{1,0:T(8,128)(2,1)S(1)} %collective-permute-done.2.rows_ref), channel_id=1, source_target_pairs={{0,2},{1,3},{2,0},{3,1},{4,6},{5,7},{6,4},{7,5},{8,10},{9,11},{10,... | collective-permute-start | bytes 184328 | tf_op jit(solution)/shard_map/ppermute | solution.py:227
  9.0 0.7 %tokens.1.tokens_ref = s32[4,32]{1,0:T(4,128)S(1)} custom-call(s32[4,32]{1,0:T(4,128)} %bitcast.10), custom_call_target="tpu_custom_call" | custom-call | flops 3000000000 | tf_op jit(solution)/shard_map/tokens/pallas_call | solution.py:230
  9.8 0.0 slice-done
  9.8 0.3 %slice-done.1 = s8[524288]{0:T(1024)(128)(4,1)S(1)} async-done(((s8[4718592]{0:T(1024)(128)(4,1)}), s8[524288]{0:T(1024)(128)(4,1)S(1)}, s32[]{:S(2)}) %slice-start.1) | async-done | bytes 524312
  10.1 1.1 %own_rows.1.before_ref = f32[2,2,128]{2,1,0:T(2,128)S(1)} custom-call(bf16[80,4608]{1,0:T(8,128)(2,1)S(1)} %copy-done, bf16[4608,512]{1,0:T(8,128)(2,1)S(1)} %bitcast.7, s32[4,32]{1,0:T(4,128)S(1)} %tokens.1.tokens_ref), custom_call_target="tpu_custom_call" | custom-call | flops 377487360 | bytes 5455872 | tf_op jit(solution)/shard_map/own_rows/pallas_call | solution.py:240
  11.2 0.0 collective-permute-done.1.other_ref
  11.2 0.4 %begin.1.before_ref = f32[80,512]{1,0:T(8,128)S(1)} custom-call(bf16[40,768]{1,0:T(8,128)(2,1)S(1)} %collective-permute-done.2.rows_ref, bf16[4608,512]{1,0:T(8,128)(2,1)S(1)} %bitcast.7, bf16[4608,512]{1,0:T(8,128)(2,1)S(1)} %collective-permute-done.1.other_ref), custom_call_target="tpu_custom_call" | custom-call | flops 94371840 | bytes 1363968 | tf_op jit(solution)/shard_map/begin/pallas_call | solution.py:257
  11.6 1.2 %collective-permute-done.4.rows_ref = bf16[40,2048]{1,0:T(8,128)(2,1)S(1)} collective-permute-done((bf16[40,2048]{1,0:T(8,128)(2,1)S(1)}, bf16[40,2048]{1,0:T(8,128)(2,1)S(1)}, u32[]{:S(2)}, u32[]{:S(2)}) %collective-permute-start.4) | collective-permute-done | bytes 163872 | tf_op jit(solution)/shard_map/ppermute | solution.py:225
  12.8 0.8 %near.1.before_ref = f32[80,512]{1,0:T(8,128)S(1)} custom-call(bf16[40,2048]{1,0:T(8,128)(2,1)S(1)} %collective-permute-done.4.rows_ref, bf16[4608,512]{1,0:T(8,128)(2,1)S(1)} %bitcast.7, bf16[4608,512]{1,0:T(8,128)(2,1)S(1)} %collective-permute-done.1.other_ref, f32[80,512]{1,0:T(8,128)S(1)} %begin.1.before_ref), custom_call_target="tpu_custom_call" | custom-call | flops 94371840 | bytes 1363968 | tf_op jit(solution)/shard_map/near/pallas_call | solution.py:259
  13.6 0.0 collective-permute-done.3.rows_ref
  13.6 0.4 %middle.1.logits_ref = f32[80,512]{1,0:T(8,128)S(1)} custom-call(bf16[40,768]{1,0:T(8,128)(2,1)S(1)} %collective-permute-done.3.rows_ref, bf16[4608,512]{1,0:T(8,128)(2,1)S(1)} %bitcast.7, bf16[4608,512]{1,0:T(8,128)(2,1)S(1)} %collective-permute-done.1.other_ref, f32[80,512]{1,0:T(8,128)S(1)} %near.1.before_ref), custom_call_target="tpu_custom_call" | custom-call | flops 94371840 | bytes 1363968 | tf_op jit(solution)/shard_map/middle/pallas_call | solution.py:261
  14.0 0.0 copy-start.1
  14.0 0.0 collective-permute-done.late_ref
  14.0 0.6 %far.1 = f32[32,2,128]{2,1,0:T(2,128)S(1)} custom-call(bf16[40,1024]{1,0:T(8,128)(2,1)S(1)} %collective-permute-done.late_ref, bf16[4608,512]{1,0:T(8,128)(2,1)S(1)} %bitcast.7, bf16[4608,512]{1,0:T(8,128)(2,1)S(1)} %collective-permute-done.1.other_ref, f32[80,512]{1,0:T(8,128)S(1)} %middle.1.logits_ref, s32[4,32]{1,0:T(4,128)S(1)} %tokens.1.tokens_ref, ...), custom_call_target="tpu_custom_call" | custom-call | flops 94371840 | bytes 1363968 | tf_op jit(solution)/shard_map/far/pallas_call | solution.py:263
  14.6 12.9 %all_to_all.5.parts_ref = f32[32,2,128]{2,1,0:T(2,128)S(1)} all-to-all(f32[32,2,128]{2,1,0:T(2,128)S(1)} %far.1), channel_id=1, replica_groups=mesh['dp'=2,'vocab'=16] {'dp','vocab'}, dimensions={0} | all-to-all | bytes 65536 | tf_op jit(solution)/shard_map/all_to_all | solution.py:275
  27.6 0.7 %tail.1 = (f32[5,16]{1,0:T(8,128)}, f32[4,16]{1,0:T(4,128)}, f32[1,16]{1,0:T(1,128)}, f32[1,1]{1,0:T(1,128)}) custom-call(f32[32,2,128]{2,1,0:T(2,128)S(1)} %all_to_all.5.parts_ref, s32[4,16]{1,0:T(4,128)S(1)} %bitcast.8), custom_call_target="tpu_custom_call" | custom-call | tf_op jit(solution)/shard_map/tail/pallas_call | solution.py:276
  (5 shorter events, 0.0 us)
Async XLA Ops:
  0.6 4.1 %copy-start = (bf16[80,4608]{1,0:T(8,128)(2,1)S(1)}, bf16[80,4608]{1,0:T(8,128)(2,1)}, u32[]{:S(2)}) copy-start(bf16[80,4608]{1,0:T(8,128)(2,1)} %hidden_ref.5) | copy-start | bytes 2211844
  0.6 10.5 %collective-permute-start.1 = (bf16[4608,512]{1,0:T(8,128)(2,1)}, bf16[4608,512]{1,0:T(8,128)(2,1)S(1)}, u32[]{:S(2)}, u32[]{:S(2)}) collective-permute-start(bf16[4608,512]{1,0:T(8,128)(2,1)} %weight_ref.9), channel_id=1, source_target_pairs={{0,1},{1,0},{2,3},{3,2},{4,5},{5,4},{6,7},{7,6},{8,9},{9,8},{10,11... | collective-permute-start | bytes 14155784 | tf_op jit(solution)/shard_map/ppermute | solution.py:229
  2.0 5.2 %collective-permute-start.2 = (bf16[40,768]{1,0:T(8,128)(2,1)S(1)}, bf16[40,768]{1,0:T(8,128)(2,1)S(1)}, u32[]{:S(2)}, u32[]{:S(2)}) collective-permute-start(bf16[40,768]{1,0:T(8,128)(2,1)S(1)} %first_piece.1), channel_id=1, source_target_pairs={{0,16},{16,0},{1,17},{17,1},{2,18},{18,2},{3,19},{19,3},{4,20},{20... | collective-permute-start | bytes 184328 | tf_op jit(solution)/shard_map/ppermute | solution.py:224
  4.7 5.1 %slice-start = ((s8[4718592]{0:T(1024)(128)(4,1)}), s8[4194304]{0:T(1024)(128)(4,1)S(1)}, s32[]{:S(2)}) async-start(s8[4718592]{0:T(1024)(128)(4,1)} %bitcast.6), calls=%async_computation.1 | async-start | bytes 8388608
  4.7 9.3 %collective-permute-start = (bf16[40,1024]{1,0:T(8,128)(2,1)S(1)}, bf16[40,1024]{1,0:T(8,128)(2,1)S(1)}, u32[]{:S(2)}, u32[]{:S(2)}) collective-permute-start(bf16[40,1024]{1,0:T(8,128)(2,1)S(1)} %get-tuple-element.10), channel_id=1, source_target_pairs={{0,16},{16,0},{1,17},{17,1},{2,18},{18,2},{3,19},{19,3},{4,20},{20... | collective-permute-start | bytes 245768 | tf_op jit(solution)/shard_map/ppermute | solution.py:226
  4.8 7.9 %collective-permute-start.4 = (bf16[40,2048]{1,0:T(8,128)(2,1)S(1)}, bf16[40,2048]{1,0:T(8,128)(2,1)S(1)}, u32[]{:S(2)}, u32[]{:S(2)}) collective-permute-start(bf16[40,2048]{1,0:T(8,128)(2,1)S(1)} %get-tuple-element.11), channel_id=1, source_target_pairs={{0,16},{16,0},{1,17},{17,1},{2,18},{18,2},{3,19},{19,3},{4,20},{20... | collective-permute-start | bytes 491528 | tf_op jit(solution)/shard_map/ppermute | solution.py:225
  7.3 6.3 %collective-permute-start.3 = (bf16[40,768]{1,0:T(8,128)(2,1)S(1)}, bf16[40,768]{1,0:T(8,128)(2,1)S(1)}, u32[]{:S(2)}, u32[]{:S(2)}) collective-permute-start(bf16[40,768]{1,0:T(8,128)(2,1)S(1)} %collective-permute-done.2.rows_ref), channel_id=1, source_target_pairs={{0,2},{1,3},{2,0},{3,1},{4,6},{5,7},{6,4},{7,5},{8,10},{9,11},{10,... | collective-permute-start | bytes 184328 | tf_op jit(solution)/shard_map/ppermute | solution.py:227
  9.0 1.1 %slice-start.1 = ((s8[4718592]{0:T(1024)(128)(4,1)}), s8[524288]{0:T(1024)(128)(4,1)S(1)}, s32[]{:S(2)}) async-start(s8[4718592]{0:T(1024)(128)(4,1)} %bitcast.6), calls=%async_computation.2 | async-start | bytes 1048576
  14.0 13.6 %copy-start.1 = (s32[16,4]{0,1:T(4,128)S(1)}, s32[16,4]{0,1:T(4,128)}, u32[]{:S(2)}) copy-start(s32[16,4]{0,1:T(4,128)} %param.7) | copy-start | bytes 772

commit v7 on v6

--- a/solution.py
+++ b/solution.py
@@ -16,7 +16,8 @@
 SUBLANES = 8
 GRANT = 16 * 2**20
 RELAYED = 6 * LANES
-EARLY = 16 * LANES
+EARLY = 9 * LANES
+NEXT = 7 * LANES
 HIDDEN_HINT = 1_200_000_000
 WEIGHT_HINT = 3_000_000_000
 VMEM = pl.BlockSpec(memory_space=pltpu.VMEM)
@@ -74,7 +75,7 @@
 
 def place(piece, other_row):
     if piece:
-        return 2 * RELAYED + (piece - 1) * EARLY
+        return 2 * RELAYED + (0, EARLY, EARLY + NEXT)[piece - 1]
     row = lax.rem(lax.axis_index("vocab") // 2 + other_row, 2)
     return pl.multiple_of(row * RELAYED, LANES)
 
@@ -135,7 +136,7 @@
     source = lax.rem(lax.axis_index("dp") + dp - shift, dp)
     core = lax.rem(lax.axis_index("vocab"), 2)
     shard = lax.axis_index("dp") * lax.axis_size("vocab") + lax.axis_index("vocab")
-    logits = logits_ref[...] + product(late_ref, (weight_ref, other_ref), 2, 0)
+    logits = logits_ref[...] + product(late_ref, (weight_ref, other_ref), 3, 0)
     blocks = [(logits[:rows], shard), (logits[rows:], shard + 1 - 2 * core)]
     seqs = rows // POSITIONS
     totals, picks = contribution(blocks, tokens_ref[...], 2 * seqs, (2 * source + core) * seqs, core * seqs)
@@ -188,7 +189,7 @@
     rows, depth = hidden.shape
     width = head_weight.shape[1]
     seqs, own_seqs = drafts.shape[0], rows // POSITIONS
-    late_size = depth - 2 * RELAYED - EARLY
+    late_size = depth - 2 * RELAYED - EARLY - NEXT
     half = rows // 2
     lines = payload_lines(seqs, own_seqs)
     params = pltpu.CompilerParams(vmem_limit_bytes=GRANT)
@@ -210,11 +211,11 @@
         compiler_params=params,
         name="first_piece",
     )(pltpu.with_memory_space_constraint(hidden, pltpu.HBM))
-    early_piece, late_piece = pl.pallas_call(
+    early_piece, next_piece, late_piece = pl.pallas_call(
         pieces_kernel,
-        out_shape=[jax.ShapeDtypeStruct((half, size), hidden.dtype) for size in (EARLY, late_size)],
+        out_shape=[jax.ShapeDtypeStruct((half, size), hidden.dtype) for size in (EARLY, NEXT, late_size)],
         in_specs=[VMEM],
-        out_specs=[VMEM] * 2,
+        out_specs=[VMEM] * 3,
         compiler_params=params,
         name="pieces",
     )(hidden)
@@ -223,6 +224,7 @@
         shift = [(i, (i + k) % dp) for i in range(dp)]
         first = lax.ppermute(first_piece, "dp", shift)
         early = lax.ppermute(early_piece, "dp", shift)
+        following = lax.ppermute(next_piece, "dp", shift)
         late = lax.ppermute(late_piece, "dp", shift)
         relayed = lax.ppermute(first, "vocab", relay)
         if k == 1:
@@ -257,6 +259,8 @@
         logits = call(first, head_weight, other_weight)
         call = multiply(functools.partial(add_kernel, 1, 0), in_specs=[VMEM] * 4, name="near")
         logits = call(early, head_weight, other_weight, logits)
+        call = multiply(functools.partial(add_kernel, 2, 0), in_specs=[VMEM] * 4, name="next")
+        logits = call(following, head_weight, other_weight, logits)
         call = multiply(functools.partial(add_kernel, 0, 1), in_specs=[VMEM] * 4, name="middle")
         logits = call(relayed, head_weight, other_weight, logits)
         count = dp * vocab if k == dp - 1 else dp
@@ -270,8 +274,8 @@
             name="far",
         )(late, head_weight, other_weight, logits, tokens, parts)
         if k < dp - 1:
-            pieces = first_piece, early_piece, late_piece
-            (first_piece, early_piece, late_piece), parts = lax.optimization_barrier((pieces, parts))
+            pieces = first_piece, early_piece, next_piece, late_piece
+            (first_piece, early_piece, next_piece, late_piece), parts = lax.optimization_barrier((pieces, parts))
     parts = lax.all_to_all(parts, ("dp", "vocab"), 0, 0)
     log_norm, logprob, expected, loss = pl.pallas_call(
         functools.partial(tail_kernel, seqs),

time: 28.5 us -> 29 us (1.018)
  local copies, waits for them, and re-layouts: 0.31 us -> 1.13 us
  blocking collectives: 12.9 us -> 12.1 us
  waiting for transfers between devices: 1.68 us -> 2.23 us
  Pallas kernels: 5.58 us -> 5.88 us
    ppermute x1, starting transfers between devices: 2.64 us -> 0.11 us  [local(): first = lax.ppermute(first_piece, 'dp', shift)]
    ppermute x1, starting transfers between devices: 0.13 us -> 2.56 us  [local(): late = lax.ppermute(late_piece, 'dp', shift)]
    ppermute x0 -> x1, starting transfers between devices: none -> 1.98 us  [local(): following = lax.ppermute(next_piece, 'dp', shift)]
    ppermute x1, starting transfers between devices: 1.96 us -> 0.08 us  [local(): early = lax.ppermute(early_piece, 'dp', shift)]
    ppermute x1, waiting for transfers between devices: 0.47 us -> 1.97 us  [local(): first = lax.ppermute(first_piece, 'dp', shift)]
    ppermute x1, waiting for transfers between devices: 1.2 us -> 0.02 us  [local(): early = lax.ppermute(early_piece, 'dp', shift)]
    all_to_all x1, blocking collectives: 12.9 us -> 12.1 us  [local(): parts = lax.all_to_all(parts, ('dp', 'vocab'), 0, 0)]
    unnamed x8 -> x10, local copies, waits for them, and re-layouts: 0.31 us -> 1.13 us
  transfers between devices with their start and end apart: 5 -> 6, of which waited for: 2 -> 2; matrix products, arithmetic and copies ran while one was open for 0% -> 0% of each run, Pallas kernels for 15% -> 16%
where the time goes in v7:
time: 29 us; the launch traced here: 28.8 us
  blocking collectives  12.1 us (42%)
  starting transfers between devices  6.8 us (23%)
  Pallas kernels  5.88 us (20%)
  waiting for transfers between devices  2.23 us (8%)
  local copies, waits for them, and re-layouts  1.13 us (4%)
  between operations  0.74 us (3%)
    all_to_all x1, blocking collectives, local(): parts = lax.all_to_all(parts, ('dp', 'vocab'), 0, 0)  12.1 us
    ppermute x1, starting transfers between devices, local(): late = lax.ppermute(late_piece, 'dp', shift)  2.56 us
    ppermute x1, starting transfers between devices, local(): following = lax.ppermute(next_piece, 'dp', shift)  1.98 us
    ppermute x1, waiting for transfers between devices, local(): first = lax.ppermute(first_piece, 'dp', shift)  1.97 us
    ppermute x1, starting transfers between devices, local(): relayed = lax.ppermute(first, 'vocab', relay)  1.52 us
    unnamed x10, local copies, waits for them, and re-layouts  1.13 us
    pallas_call x1, Pallas kernels, local(): pl.pallas_call(own_kernel, out_shape=jax.ShapeDtypeStruct((dp, lines, LAN...  1.07 us
    pallas_call x1, Pallas kernels, local(): pl.pallas_call(first_kernel, out_shape=jax.ShapeDtypeStruct((half, RELAYE...  0.99 us
  transfers between devices with their start and end apart: 6, of which 2 were waited for; matrix products, arithmetic and copies ran while one was open for 0% of the time, Pallas kernels for 16%

profile of v7, /device:TPU:0, one launch (start us, length us, event | category | flops | bytes accessed | tf_op | source)
XLA Modules:
  0.0 28.8 jit_solution(17840089175744799931)
XLA Ops:
  0.6 0.6 %collective-permute-start.1 = (bf16[4608,512]{1,0:T(8,128)(2,1)}, bf16[4608,512]{1,0:T(8,128)(2,1)S(1)}, u32[]{:S(2)}, u32[]{:S(2)}) collective-permute-start(bf16[4608,512]{1,0:T(8,128)(2,1)} %weight_ref.11), channel_id=1, source_target_pairs={{0,1},{1,0},{2,3},{3,2},{4,5},{5,4},{6,7},{7,6},{8,9},{9,8},{10,11... | collective-permute-start | bytes 14155784 | tf_op jit(solution)/shard_map/ppermute | solution.py:231
  1.2 1.1 %copy-done = bf16[80,4608]{1,0:T(8,128)(2,1)S(1)} copy-done((bf16[80,4608]{1,0:T(8,128)(2,1)S(1)}, bf16[80,4608]{1,0:T(8,128)(2,1)}, u32[]{:S(2)}) %copy-start) | copy-done | bytes 737304
  2.3 2.6 %collective-permute-start = (bf16[40,1024]{1,0:T(8,128)(2,1)S(1)}, bf16[40,1024]{1,0:T(8,128)(2,1)S(1)}, u32[]{:S(2)}, u32[]{:S(2)}) collective-permute-start(bf16[40,1024]{1,0:T(8,128)(2,1)S(1)} %get-tuple-element.11), channel_id=1, source_target_pairs={{0,16},{16,0},{1,17},{17,1},{2,18},{18,2},{3,19},{19,3},{4,20},{20... | collective-permute-start | bytes 245768 | tf_op jit(solution)/shard_map/ppermute | solution.py:228
  4.9 1.0 %first_piece.1 = bf16[40,768]{1,0:T(8,128)(2,1)S(1)} custom-call(bf16[80,4608]{1,0:T(8,128)(2,1)} %hidden_ref.5), custom_call_target="tpu_custom_call" | custom-call | flops 1200000000 | tf_op jit(solution)/shard_map/first_piece/pallas_call | solution.py:204
  5.9 0.1 collective-permute-start.2
  6.0 2.0 %collective-permute-start.4 = (bf16[40,896]{1,0:T(8,128)(2,1)S(1)}, bf16[40,896]{1,0:T(8,128)(2,1)S(1)}, u32[]{:S(2)}, u32[]{:S(2)}) collective-permute-start(bf16[40,896]{1,0:T(8,128)(2,1)S(1)} %get-tuple-element.12), channel_id=1, source_target_pairs={{0,16},{16,0},{1,17},{17,1},{2,18},{18,2},{3,19},{19,3},{4,20},{20... | collective-permute-start | bytes 215048 | tf_op jit(solution)/shard_map/ppermute | solution.py:227
  8.0 0.1 collective-permute-start.5
  8.1 0.8 %tokens.1.tokens_ref = s32[4,32]{1,0:T(4,128)S(1)} custom-call(s32[4,32]{1,0:T(4,128)} %bitcast.10), custom_call_target="tpu_custom_call" | custom-call | flops 3000000000 | tf_op jit(solution)/shard_map/tokens/pallas_call | solution.py:232
  8.9 2.0 %collective-permute-done.2.rows_ref = bf16[40,768]{1,0:T(8,128)(2,1)S(1)} collective-permute-done((bf16[40,768]{1,0:T(8,128)(2,1)S(1)}, bf16[40,768]{1,0:T(8,128)(2,1)S(1)}, u32[]{:S(2)}, u32[]{:S(2)}) %collective-permute-start.2) | collective-permute-done | bytes 61472 | tf_op jit(solution)/shard_map/ppermute | solution.py:225
  10.8 1.5 %collective-permute-start.3 = (bf16[40,768]{1,0:T(8,128)(2,1)S(1)}, bf16[40,768]{1,0:T(8,128)(2,1)S(1)}, u32[]{:S(2)}, u32[]{:S(2)}) collective-permute-start(bf16[40,768]{1,0:T(8,128)(2,1)S(1)} %collective-permute-done.2.rows_ref), channel_id=1, source_target_pairs={{0,2},{1,3},{2,0},{3,1},{4,6},{5,7},{6,4},{7,5},{8,10},{9,11},{10,... | collective-permute-start | bytes 184328 | tf_op jit(solution)/shard_map/ppermute | solution.py:229
  12.4 1.1 %own_rows.1.before_ref = f32[2,2,128]{2,1,0:T(2,128)S(1)} custom-call(bf16[80,4608]{1,0:T(8,128)(2,1)S(1)} %copy-done.1, bf16[4608,512]{1,0:T(8,128)(2,1)S(1)} %bitcast.7, s32[4,32]{1,0:T(4,128)S(1)} %tokens.1.tokens_ref), custom_call_target="tpu_custom_call" | custom-call | flops 377487360 | bytes 5455872 | tf_op jit(solution)/shard_map/own_rows/pallas_call | solution.py:242
  13.4 0.0 collective-permute-done.1.other_ref
  13.4 0.4 %begin.1.before_ref = f32[80,512]{1,0:T(8,128)S(1)} custom-call(bf16[40,768]{1,0:T(8,128)(2,1)S(1)} %collective-permute-done.2.rows_ref, bf16[4608,512]{1,0:T(8,128)(2,1)S(1)} %bitcast.7, bf16[4608,512]{1,0:T(8,128)(2,1)S(1)} %collective-permute-done.1.other_ref), custom_call_target="tpu_custom_call" | custom-call | flops 94371840 | bytes 1363968 | tf_op jit(solution)/shard_map/begin/pallas_call | solution.py:259
  13.8 0.0 collective-permute-done.5.rows_ref
  13.8 0.5 %near.1.before_ref = f32[80,512]{1,0:T(8,128)S(1)} custom-call(bf16[40,1152]{1,0:T(8,128)(2,1)S(1)} %collective-permute-done.5.rows_ref, bf16[4608,512]{1,0:T(8,128)(2,1)S(1)} %bitcast.7, bf16[4608,512]{1,0:T(8,128)(2,1)S(1)} %collective-permute-done.1.other_ref, f32[80,512]{1,0:T(8,128)S(1)} %begin.1.before_ref), custom_call_target="tpu_custom_call" | custom-call | flops 94371840 | bytes 1363968 | tf_op jit(solution)/shard_map/near/pallas_call | solution.py:261
  14.4 0.0 collective-permute-done.4.rows_ref
  14.4 0.4 %next.1.before_ref = f32[80,512]{1,0:T(8,128)S(1)} custom-call(bf16[40,896]{1,0:T(8,128)(2,1)S(1)} %collective-permute-done.4.rows_ref, bf16[4608,512]{1,0:T(8,128)(2,1)S(1)} %bitcast.7, bf16[4608,512]{1,0:T(8,128)(2,1)S(1)} %collective-permute-done.1.other_ref, f32[80,512]{1,0:T(8,128)S(1)} %near.1.before_ref), custom_call_target="tpu_custom_call" | custom-call | flops 94371840 | bytes 1363968 | tf_op jit(solution)/shard_map/next/pallas_call | solution.py:263
  14.8 0.2 collective-permute-done.3.rows_ref
  15.0 0.4 %middle.1.logits_ref = f32[80,512]{1,0:T(8,128)S(1)} custom-call(bf16[40,768]{1,0:T(8,128)(2,1)S(1)} %collective-permute-done.3.rows_ref, bf16[4608,512]{1,0:T(8,128)(2,1)S(1)} %bitcast.7, bf16[4608,512]{1,0:T(8,128)(2,1)S(1)} %collective-permute-done.1.other_ref, f32[80,512]{1,0:T(8,128)S(1)} %next.1.before_ref), custom_call_target="tpu_custom_call" | custom-call | flops 94371840 | bytes 1363968 | tf_op jit(solution)/shard_map/middle/pallas_call | solution.py:265
  15.4 0.0 copy-start.2
  15.4 0.0 collective-permute-done.late_ref
  15.5 0.6 %far.1 = f32[32,2,128]{2,1,0:T(2,128)S(1)} custom-call(bf16[40,1024]{1,0:T(8,128)(2,1)S(1)} %collective-permute-done.late_ref, bf16[4608,512]{1,0:T(8,128)(2,1)S(1)} %bitcast.7, bf16[4608,512]{1,0:T(8,128)(2,1)S(1)} %collective-permute-done.1.other_ref, f32[80,512]{1,0:T(8,128)S(1)} %middle.1.logits_ref, s32[4,32]{1,0:T(4,128)S(1)} %tokens.1.tokens_ref, ...), custom_call_target="tpu_custom_call" | custom-call | flops 94371840 | bytes 1363968 | tf_op jit(solution)/shard_map/far/pallas_call | solution.py:267
  16.1 12.1 %all_to_all.5.parts_ref = f32[32,2,128]{2,1,0:T(2,128)S(1)} all-to-all(f32[32,2,128]{2,1,0:T(2,128)S(1)} %far.1), channel_id=1, replica_groups=mesh['dp'=2,'vocab'=16] {'dp','vocab'}, dimensions={0} | all-to-all | bytes 65536 | tf_op jit(solution)/shard_map/all_to_all | solution.py:279
  28.1 0.7 %tail.1 = (f32[5,16]{1,0:T(8,128)}, f32[4,16]{1,0:T(4,128)}, f32[1,16]{1,0:T(1,128)}, f32[1,1]{1,0:T(1,128)}) custom-call(f32[32,2,128]{2,1,0:T(2,128)S(1)} %all_to_all.5.parts_ref, s32[4,16]{1,0:T(4,128)S(1)} %bitcast.8), custom_call_target="tpu_custom_call" | custom-call | tf_op jit(solution)/shard_map/tail/pallas_call | solution.py:280
  (10 shorter events, 0.0 us)
Async XLA Ops:
  0.6 12.8 %collective-permute-start.1 = (bf16[4608,512]{1,0:T(8,128)(2,1)}, bf16[4608,512]{1,0:T(8,128)(2,1)S(1)}, u32[]{:S(2)}, u32[]{:S(2)}) collective-permute-start(bf16[4608,512]{1,0:T(8,128)(2,1)} %weight_ref.11), channel_id=1, source_target_pairs={{0,1},{1,0},{2,3},{3,2},{4,5},{5,4},{6,7},{7,6},{8,9},{9,8},{10,11... | collective-permute-start | bytes 14155784 | tf_op jit(solution)/shard_map/ppermute | solution.py:231
  1.2 1.1 %copy-start = (bf16[80,4608]{1,0:T(8,128)(2,1)S(1)}, bf16[80,4608]{1,0:T(8,128)(2,1)}, u32[]{:S(2)}) copy-start(bf16[80,4608]{1,0:T(8,128)(2,1)} %hidden_ref.5) | copy-start | bytes 2211844
  2.3 13.1 %collective-permute-start = (bf16[40,1024]{1,0:T(8,128)(2,1)S(1)}, bf16[40,1024]{1,0:T(8,128)(2,1)S(1)}, u32[]{:S(2)}, u32[]{:S(2)}) collective-permute-start(bf16[40,1024]{1,0:T(8,128)(2,1)S(1)} %get-tuple-element.11), channel_id=1, source_target_pairs={{0,16},{16,0},{1,17},{17,1},{2,18},{18,2},{3,19},{19,3},{4,20},{20... | collective-permute-start | bytes 245768 | tf_op jit(solution)/shard_map/ppermute | solution.py:228
  4.9 7.5 %slice-start = ((s8[4718592]{0:T(1024)(128)(4,1)}), s8[4194304]{0:T(1024)(128)(4,1)S(1)}, s32[]{:S(2)}) async-start(s8[4718592]{0:T(1024)(128)(4,1)} %bitcast.6), calls=%async_computation.1 | async-start | bytes 8388608
  5.9 4.9 %collective-permute-start.2 = (bf16[40,768]{1,0:T(8,128)(2,1)S(1)}, bf16[40,768]{1,0:T(8,128)(2,1)S(1)}, u32[]{:S(2)}, u32[]{:S(2)}) collective-permute-start(bf16[40,768]{1,0:T(8,128)(2,1)S(1)} %first_piece.1), channel_id=1, source_target_pairs={{0,16},{16,0},{1,17},{17,1},{2,18},{18,2},{3,19},{19,3},{4,20},{20... | collective-permute-start | bytes 184328 | tf_op jit(solution)/shard_map/ppermute | solution.py:225
  6.0 8.4 %collective-permute-start.4 = (bf16[40,896]{1,0:T(8,128)(2,1)S(1)}, bf16[40,896]{1,0:T(8,128)(2,1)S(1)}, u32[]{:S(2)}, u32[]{:S(2)}) collective-permute-start(bf16[40,896]{1,0:T(8,128)(2,1)S(1)} %get-tuple-element.12), channel_id=1, source_target_pairs={{0,16},{16,0},{1,17},{17,1},{2,18},{18,2},{3,19},{19,3},{4,20},{20... | collective-permute-start | bytes 215048 | tf_op jit(solution)/shard_map/ppermute | solution.py:227
  8.0 5.9 %collective-permute-start.5 = (bf16[40,1152]{1,0:T(8,128)(2,1)S(1)}, bf16[40,1152]{1,0:T(8,128)(2,1)S(1)}, u32[]{:S(2)}, u32[]{:S(2)}) collective-permute-start(bf16[40,1152]{1,0:T(8,128)(2,1)S(1)} %get-tuple-element.13), channel_id=1, source_target_pairs={{0,16},{16,0},{1,17},{17,1},{2,18},{18,2},{3,19},{19,3},{4,20},{20... | collective-permute-start | bytes 276488 | tf_op jit(solution)/shard_map/ppermute | solution.py:226
  8.1 4.3 %slice-start.1 = ((s8[4718592]{0:T(1024)(128)(4,1)}), s8[524288]{0:T(1024)(128)(4,1)S(1)}, s32[]{:S(2)}) async-start(s8[4718592]{0:T(1024)(128)(4,1)} %bitcast.6), calls=%async_computation.2 | async-start | bytes 1048576
  8.1 4.3 %copy-start.1 = (bf16[80,4608]{1,0:T(8,128)(2,1)S(1)}, bf16[80,4608]{1,0:T(8,128)(2,1)}, u32[]{:S(2)}) copy-start(bf16[80,4608]{1,0:T(8,128)(2,1)} %hidden_ref.5) | copy-start | bytes 2211844
  10.8 4.2 %collective-permute-start.3 = (bf16[40,768]{1,0:T(8,128)(2,1)S(1)}, bf16[40,768]{1,0:T(8,128)(2,1)S(1)}, u32[]{:S(2)}, u32[]{:S(2)}) collective-permute-start(bf16[40,768]{1,0:T(8,128)(2,1)S(1)} %collective-permute-done.2.rows_ref), channel_id=1, source_target_pairs={{0,2},{1,3},{2,0},{3,1},{4,6},{5,7},{6,4},{7,5},{8,10},{9,11},{10,... | collective-permute-start | bytes 184328 | tf_op jit(solution)/shard_map/ppermute | solution.py:229
  15.4 12.7 %copy-start.2 = (s32[16,4]{0,1:T(4,128)S(1)}, s32[16,4]{0,1:T(4,128)}, u32[]{:S(2)}) copy-start(s32[16,4]{0,1:T(4,128)} %param.7) | copy-start | bytes 772
